TPU v7x, 32 devices: a whole 2x2x4 slice. The times are simulated.
32 devices in a mesh: gx: 16 (over z, y, x), gy: 2 (over core).
Axes of the slice: x: 2, y: 2, z: 4, core: 2. Of those that a mesh axis runs over, the one named last changes fastest.
Arguments:
- moisture_ratio: float32 [2, 128, 256], P(None, 'gx', 'gy'), may hold values from 11 to 14
- kelvin_warmth: float32 [2, 128, 256], P(None, 'gx', 'gy'), may hold values from 286 to 292
- droplet_size_micron: float32 [8, 2, 128, 256], P(None, None, 'gx', 'gy'), may hold values from 0.5 to 25
- weighting_factor: float32 [8, 2, 128, 256], P(None, None, 'gx', 'gy'), may hold values from 0.1 to 2
- dry_nucleus_size: float32 [8, 2, 128, 256], P(None, None, 'gx', 'gy'), may hold values from 0.02 to 0.3
- fractional_offset_east: float32 [8, 2, 128, 256], P(None, None, 'gx', 'gy'), may hold values from 0 to 1
- fractional_offset_north: float32 [8, 2, 128, 256], P(None, None, 'gx', 'gy'), may hold values from 0 to 1
- encounter_permutation: int32 [8, 2, 128, 256], P(None, None, 'gx', 'gy'), may hold values from 0 to 7, as said below
- departing_eastwest_lists: int32 [16, 2, 2048], P('gx', None, 'gy'), may hold values from -1 to 16383, as said below
- departing_northsouth_lists: int32 [16, 2, 96], P('gx', None, 'gy'), may hold values from -1 to 16383, as said below
- departing_diagonal_lists: int32 [16, 4, 16], P('gx', None, 'gy'), may hold values from -1 to 16383, as said below
Outputs:
- resulting_moisture_ratio: float32 [2, 128, 256], P(None, 'gx', 'gy')
- resulting_kelvin_value: float32 [2, 128, 256], P(None, 'gx', 'gy')
- resulting_droplet_size: float32 [8, 2, 128, 256], P(None, None, 'gx', 'gy')
- resulting_weighting_factor: float32 [8, 2, 128, 256], P(None, None, 'gx', 'gy')
- arrival_particle_records: float32 [5, 16, 4352], P(None, 'gx', 'gy')
- arrival_box_index: int32 [16, 4352], P('gx', 'gy')
Inputs may be any that keep to these rules, and one draw needn't show every extreme that they name: `encounter_permutation`: along the first dimension, the 8 entries of each cell are a permutation of 0 to 7. `departing_eastwest_lists`: each list holds live slot numbers of its own device first and -1 after them, at most 1024 live, and some list of some device is full. Row 0 names only droplets of cells with i = 7, row 1 only i = 0, both only 0 < j < 127. No slot is named twice among all lists of a device. `departing_northsouth_lists`: each list holds live slot numbers of its own device first and -1 after them, at most 48 live, and some list of some device is full. Row 0 names only droplets of cells with j = 127, row 1 only j = 0, both only 0 < i < 7. `departing_diagonal_lists`: each list holds live slot numbers of its own device first and -1 after them, at most 8 live, and some list of some device is full. Row r names only droplets of the corner cell that its move points to: i = 7 for rows 0 and 1, i = 0 for rows 2 and 3, j = 127 for rows 0 and 2, j = 0 for rows 1 and 3.
All inputs are finite; a program needn't handle non-finite values.
Results may differ from a plain program's by a relative error of at most 0.0003.
Values sent between devices are 32-bit elements; how exact they have to be, the bound alone decides.
A program may use at most 64 MiB of HBM per device.

v0:
```python
import functools

import jax
import jax.numpy as jnp
from jax import lax
from jax.experimental import pallas as pl
from jax.experimental.pallas import tpu as pltpu
from jax.sharding import PartitionSpec as P

NEWTON = 4
MIX_HORIZONTAL = 0.2
MIX_VERTICAL = 0.05
EXCESS_FACTOR = 4.2222
CURVATURE = 0.0012
KAPPA_SOLUTE = 0.6
GROWTH_STEP = 200.0
COLLIDE_RATE = 4e-07
VAPOUR_PER_SOURCE = 0.001
WARMING_FACTOR = 0.00249

MESH = pl.DeviceIdType.MESH
SHIFTS = (-1, 0, 1)
MOVES = (1, -1)


def div(x, n):
    return lax.shift_right_arithmetic(x, jnp.int32(n.bit_length() - 1))


def mod(x, n):
    return lax.bitwise_and(x, jnp.int32(n - 1))


def iota(shape, dim):
    return lax.broadcasted_iota(jnp.int32, shape, dim)


def turn(x, shift, dim):
    shift %= x.shape[dim]
    return pltpu.roll(x, shift, dim) if shift else x


def kernel_weights(offset):
    return {
        -1: jnp.maximum(0.5 - offset, 0.0),
        0: 1.0 - jnp.abs(offset - 0.5),
        1: jnp.maximum(offset - 0.5, 0.0),
    }


def pieces(x):
    high = x.astype(jnp.bfloat16)
    rest = x - high.astype(jnp.float32)
    middle = rest.astype(jnp.bfloat16)
    low = (rest - middle.astype(jnp.float32)).astype(jnp.bfloat16)
    return high, middle, low


def pick(tables, hot_row, hot_lane):
    rows = tables[0].shape[0]
    split = [pieces(t) for t in tables]
    stacked = jnp.concatenate([s[n] for n in range(3) for s in split], 0)
    got = jnp.dot(stacked, hot_lane, preferred_element_type=jnp.float32)
    third = rows * len(tables)
    got = (got[:third] + got[third : 2 * third]) + got[2 * third :]
    return [
        jnp.sum(jnp.where(hot_row, got[n * rows : (n + 1) * rows], 0.0), 0, keepdims=True)
        for n in range(len(tables))
    ]


def grow(radius, weight, dry, wx, wy, window):
    forcing = -CURVATURE / radius
    for a in SHIFTS:
        across = sum(wy[b] * window[a, b] for b in SHIFTS)
        forcing = forcing + wx[a] * across
    initial = radius * radius
    lowest = dry * dry
    solute = KAPPA_SOLUTE * lowest * dry
    wetted = initial
    for sweep in range(NEWTON):
        inverse_root = lax.rsqrt(wetted)
        inverse_square = inverse_root * inverse_root
        pull = solute * (inverse_square * inverse_root)
        residue = wetted - initial - GROWTH_STEP * (forcing + pull)
        slope = 1.0 + (1.5 * GROWTH_STEP) * pull * inverse_square
        wetted = jnp.maximum(wetted - residue / slope, lowest)
    root = jnp.sqrt(wetted)
    return root, weight * (wetted * root - initial * radius)


def collide(r_p, r_q, m_p, m_q, big):
    r_hi, r_lo = jnp.where(big, r_p, r_q), jnp.where(big, r_q, r_p)
    m_hi, m_lo = jnp.where(big, m_p, m_q), jnp.where(big, m_q, m_p)
    total = r_p + r_q
    rate = COLLIDE_RATE * m_hi * total * total * jnp.abs(r_p * r_p - r_q * r_q)
    chance = 1.0 - jnp.exp(-rate)
    volume = r_lo * r_lo * r_lo + chance * r_hi * r_hi * r_hi
    merged = jnp.exp(jnp.log(volume) * (1.0 / 3.0))
    return r_hi, merged, m_hi - chance * m_lo, m_lo


def body(
    sizes,
    moist_in, warm_in, size_in, mult_in, dry_in, east_in, north_in, perm_in,
    lx_in, ly_in, lc_in,
    moist_out, warm_out, size_out, mult_out, rec_out, box_out,
    state, drops, perm, lx, ly, lc,
    state_pack, state_x, state_y, state_c,
    list_pack, list_x, row_pack, row_x,
    dep_out, dep_in, edge, edge_in, mask, coal,
    in_sem, x_send, x_recv, c_send, c_recv, y_send, y_recv,
):
    levels, cx, cy, sd, kx, ky, kc, nx, ny = sizes
    me_x = lax.axis_index("gx")
    me_y = lax.axis_index("gy")
    ys = (1,) if ny == 2 else (1, -1)
    half = cx // 2

    def at(d):
        return (lax.rem(me_x + d[0] + nx, nx), lax.rem(me_y + d[1] + ny, ny))

    loads = []

    def load(source, target):
        copy = pltpu.make_async_copy(source, target, in_sem.at[len(loads)])
        copy.start()
        loads.append(copy)

    load(moist_in, state.at[0])
    load(warm_in, state.at[1])
    for n, source in enumerate((size_in, mult_in, dry_in, east_in, north_in)):
        load(source, drops.at[n])
    load(perm_in, perm)
    load(lx_in.at[0], lx)
    load(ly_in.at[0], ly)
    load(lc_in.at[0], lc)

    friends = [(dx, 0) for dx in MOVES] + [(dx, dy) for dx in MOVES for dy in ys] + [(0, dy) for dy in ys]
    barrier = pltpu.get_barrier_semaphore()
    for d in friends:
        pl.semaphore_signal(barrier, inc=1, device_id=at(d), device_id_type=MESH)

    sends = []

    def send(source, target, s_sem, r_sem, d):
        copy = pltpu.make_async_remote_copy(
            src_ref=source, dst_ref=target, send_sem=s_sem, recv_sem=r_sem,
            device_id=at(d), device_id_type=MESH,
        )
        copy.start()
        sends.append(copy)
        return copy

    line = iota((cx, cy), 0)
    lane = iota((cx, cy), 1)
    low_half = line < half

    loads[0].wait()
    loads[1].wait()
    for f in range(2):
        first, second = state[f, 0], turn(state[f, 1], half, 0)
        state_pack[0, f] = jnp.where(low_half, second, first)
        state_pack[1, f] = jnp.where(low_half, first, second)

    pl.semaphore_wait(barrier, len(friends))

    early = []
    for s, dx in enumerate(MOVES):
        early.append(send(state_pack.at[s], state_x.at[s], x_send.at[s, 0], x_recv.at[s, 0], (dx, 0)))
    for s, dx in enumerate(MOVES):
        for t, dy in enumerate(ys):
            early.append(
                send(state_pack.at[s], state_c.at[s, t], c_send.at[s, t], c_recv.at[s, t], (dx, dy))
            )
    for t, dy in enumerate(ys):
        early.append(send(state, state_y.at[t], y_send.at[t, 0], y_recv.at[t, 0], (0, dy)))

    for copy in loads[2:]:
        copy.wait()
    rows = sd * levels
    block = cx * cy
    tall = levels * cx
    lists = []
    late = []
    for s, (dx, side) in enumerate(zip(MOVES, (cx - 1, 0))):
        list_pack[s, :, 0:kx] = lx[s : s + 1, :]
        list_pack[s, :, kx:] = jnp.concatenate(
            [lc[2 * s : 2 * s + 1, :], lc[2 * s + 1 : 2 * s + 2, :], jnp.full((1, 128 - 2 * kc), -1, jnp.int32)], 1
        )
        lists.append(send(list_pack.at[s], list_x.at[s], x_send.at[s, 1], x_recv.at[s, 1], (dx, 0)))
    for s, (dx, side) in enumerate(zip(MOVES, (cx - 1, 0))):
        for l in range(levels):
            picked = pl.ds(l * cx + side, sd, stride=tall)
            for n in range(5):
                row_pack[s, n, pl.ds(l * sd, sd), :] = drops[n, picked, :]
            row_pack[s, 5, pl.ds(l * sd, sd), :] = perm[picked, :].astype(jnp.float32)
        late.append(send(row_pack.at[s], row_x.at[s], x_send.at[s, 2], x_recv.at[s, 2], (dx, 0)))

    mask[...] = jnp.zeros_like(mask)
    for r, side in enumerate((cx - 1, 0)):
        slots = lx[r : r + 1, :]
        hot_row = iota((rows, kx), 0) == div(slots, block)
        hot_lane = jnp.where(iota((cy, kx), 0) == mod(slots, cy), 1.0, 0.0).astype(jnp.bfloat16)
        named = lax.dot_general(
            jnp.where(hot_row, 1.0, 0.0).astype(jnp.bfloat16), hot_lane,
            (((1,), (1,)), ((), ())), preferred_element_type=jnp.float32,
        )
        mask[pl.ds(side, rows, stride=cx), :] = named

    width = 2 * ky + 4 * kc
    lane_e = iota((1, width), 1)
    high = (lane_e < ky) | ((lane_e >= 2 * ky) & (lane_e < 2 * ky + 2 * kc))
    high_all = jnp.broadcast_to(high, (rows * cx, width))
    slots = jnp.concatenate(
        [ly[0:1, :], ly[1:2, :], lc[0:1, :], lc[2:3, :], lc[1:2, :], lc[3:4, :]], 1
    )
    named_e = iota((rows * cx, width), 0) == div(slots, cy)
    hot_e = jnp.where(named_e, 1.0, 0.0)
    left_high = jnp.max(jnp.where(high_all, hot_e, 0.0), 1, keepdims=True)
    left_low = jnp.max(jnp.where(high_all, 0.0, hot_e), 1, keepdims=True)
    lane_all = iota((rows * cx, cy), 1)
    mask[...] = mask[...] + jnp.where(
        lane_all == cy - 1, left_high, jnp.where(lane_all == 0, left_low, 0.0)
    )
    named_y = named_e & (iota((rows * cx, width), 1) < 2 * ky)

    def pick_y(table):
        both = jnp.where(high_all, table[:, cy - 1 : cy], table[:, 0:1])
        return jnp.sum(jnp.where(named_y, both, 0.0), 0, keepdims=True)

    fixed_y = [pick_y(drops[n]) for n in (2, 3, 4)]

    for copy in lists:
        copy.wait_recv()
    hots = []
    corners = []
    for s, dx in enumerate(MOVES):
        slots = list_x[s, :, 0:kx]
        live = slots >= 0
        j = mod(slots, cy)
        level = mod(div(slots, block), levels)
        row = jnp.where(live, level * sd + div(slots, block * levels), -1)
        hot_row = iota((rows, kx), 0) == row
        hot_lane = jnp.where(iota((cy, kx), 0) == j, 1.0, 0.0).astype(jnp.bfloat16)
        hots.append((hot_row, hot_lane))
        target = (level * cx + mod(mod(div(slots, cy), cx) + dx, cx)) * cy + j
        box_out[:, pl.ds(s * kx, kx)] = jnp.where(live, target, -1)
        corners.append(list_x[s, :, kx:])
    blank = jnp.full((1, 2 * ky), -1, jnp.int32)
    corner = [c[:, n * kc : (n + 1) * kc] for n in range(2) for c in corners]
    slots = jnp.concatenate([ly[0:1, :], ly[1:2, :]] + corner, 1)
    move_y = jnp.where(high, 1, -1)
    which = div(lane_e - 2 * ky, kc)
    move_x = jnp.where(lane_e < 2 * ky, 0, jnp.where(mod(which, 2) == 0, 1, -1))
    level = mod(div(slots, block), levels)
    target = (level * cx + mod(mod(div(slots, cy), cx) + move_x, cx)) * cy + mod(mod(slots, cy) + move_y, cy)
    edge[5:6, :] = jnp.where(slots >= 0, target, -1).astype(jnp.float32)
    edge[6:8, :] = jnp.zeros((2, width), jnp.float32)
    row = jnp.where((slots >= 0) & (lane_e >= 2 * ky), level * sd + div(slots, block * levels), -1)
    named_c = [
        (iota((rows, width), 0) == row) & (mod(div(iota((rows, width), 1) - 2 * ky, kc), 2) == s) for s in range(2)
    ]
    high_c = high_all[:rows]

    def pick_c(s, table):
        both = jnp.where(high_c, table[:, cy - 1 : cy], table[:, 0:1])
        return jnp.sum(jnp.where(named_c[s], both, 0.0), 0, keepdims=True)

    for copy in early:
        copy.wait_recv()

    def blend(parts):
        return parts[0] if len(parts) == 1 else jnp.where(lane < cy // 2, parts[1], parts[0])

    wide = []
    for f in range(2):
        wide.append([])
        for l in range(levels):
            def beyond(up, down):
                return jnp.where(low_half, turn(down, half * l, 0), turn(up, half * l, 0))

            across = beyond(state_x[0, f], state_x[1, f])
            far = blend([beyond(state_c[0, t, f], state_c[1, t, f]) for t in range(len(ys))])
            side_y = blend([state_y[t, f, l] for t in range(len(ys))])
            own_half = jnp.concatenate([state[f, l], across], 0)
            wide[f].append(jnp.concatenate([own_half, jnp.concatenate([side_y, far], 0)], 1))
    mixed = []
    for f in range(2):
        mixed.append([])
        for l in range(levels):
            centre = wide[f][l]
            horizontal = (
                turn(centre, -1, 0) + turn(centre, 1, 0) + turn(centre, -1, 1) + turn(centre, 1, 1)
                - 4.0 * centre
            )
            vertical = wide[f][min(l + 1, levels - 1)] + wide[f][max(l - 1, 0)] - 2.0 * centre
            mixed[f].append(centre + MIX_HORIZONTAL * horizontal + MIX_VERTICAL * vertical)
    window = {(a, b): [] for a in SHIFTS for b in SHIFTS}
    beside = [[{}, {}] for l in range(levels)]
    for l in range(levels):
        vapour, warmth = mixed[0][l], mixed[1][l]
        humid = vapour / (
            EXCESS_FACTOR * jnp.exp(17.27 * (warmth - 273.15) / (warmth - 35.86))
        ) - 1.0
        for b in SHIFTS:
            column = turn(humid, -b, 1)[:, :cy]
            for a in SHIFTS:
                window[a, b].append(turn(column, -a, 0)[:cx])
                for s, home in enumerate((2 * cx - 1, cx)):
                    r = (home + a) % (2 * cx)
                    beside[l][s][a, b] = jnp.broadcast_to(column[r : r + 1], (sd, cy))
        moist_out[l] = vapour[:cx, :cy]
        warm_out[l] = warmth[:cx, :cy]
    window = {key: jnp.concatenate(parts, 0) for key, parts in window.items()}

    grown = []
    mult = []
    deposit = {}
    for k in range(sd):
        part = pl.ds(k * tall, tall)
        weight = drops[1, part, :]
        wx = kernel_weights(drops[3, part, :])
        wy = kernel_weights(drops[4, part, :])
        root, condensed = grow(drops[0, part, :], weight, drops[2, part, :], wx, wy, window)
        for a in SHIFTS:
            along = wx[a] * condensed
            for b in SHIFTS:
                term = wy[b] * along
                deposit[a, b] = term if k == 0 else deposit[a, b] + term
        grown.append(root)
        mult.append(weight)

    order = [perm[k * tall : (k + 1) * tall, :] for k in range(sd)]
    hit = [[order[p] == m for m in range(sd)] for p in range(sd)]

    def member(values, p):
        got = values[0]
        for m in range(1, sd):
            got = jnp.where(hit[p][m], values[m], got)
        return got

    after_radius = []
    after_mult = []
    for pair in range(sd // 2):
        p, q = 2 * pair, 2 * pair + 1
        m_p, m_q = member(mult, p), member(mult, q)
        big = m_p >= m_q
        kept, merged, reduced, m_lo = collide(member(grown, p), member(grown, q), m_p, m_q, big)
        after_radius += [jnp.where(big, kept, merged), jnp.where(big, merged, kept)]
        after_mult += [jnp.where(big, reduced, m_lo), jnp.where(big, m_lo, reduced)]
    for m in range(sd):
        part = pl.ds(m * tall, tall)
        radius, weight = after_radius[0], after_mult[0]
        for p in range(1, sd):
            radius = jnp.where(hit[p][m], after_radius[p], radius)
            weight = jnp.where(hit[p][m], after_mult[p], weight)
        size_out[part, :] = radius
        coal[part, :] = weight
        mult_out[part, :] = jnp.where(mask[part, :] > 0.0, 0.0, weight)

    for copy in late:
        copy.wait_recv()

    slot_k = iota((sd, cy), 0)
    even = mod(slot_k, 2) == 0
    arrive = [[{}, {}] for l in range(levels)]
    tables = [[], []]
    for s in range(2):
        parts = []
        for l in range(levels):
            radius, weight, dry, east, north, turns = (row_x[s, n, pl.ds(l * sd, sd), :] for n in range(6))
            wx, wy = kernel_weights(east), kernel_weights(north)
            root, condensed = grow(radius, weight, dry, wx, wy, beside[l][s])
            along = wx[MOVES[s]] * condensed
            for b in SHIFTS:
                arrive[l][s][b] = jnp.sum(wy[b] * along, 0, keepdims=True)

            def spot(x, m):
                return jnp.broadcast_to(x[m : m + 1], (sd, cy))

            r_p, m_p = spot(root, 0), spot(weight, 0)
            for m in range(1, sd):
                chosen = turns == float(m)
                r_p = jnp.where(chosen, spot(root, m), r_p)
                m_p = jnp.where(chosen, spot(weight, m), m_p)
            r_q = jnp.where(even, turn(r_p, -1, 0), turn(r_p, 1, 0))
            m_q = jnp.where(even, turn(m_p, -1, 0), turn(m_p, 1, 0))
            big = (m_p > m_q) | (even & (m_p == m_q))
            kept, merged, reduced, m_lo = collide(r_p, r_q, m_p, m_q, big)
            radius = jnp.where(big, kept, merged)
            weight = jnp.where(big, reduced, m_lo)
            radius_k, weight_k = spot(radius, 0), spot(weight, 0)
            wanted = slot_k.astype(jnp.float32)
            for p in range(1, sd):
                chosen = spot(turns, p) == wanted
                radius_k = jnp.where(chosen, spot(radius, p), radius_k)
                weight_k = jnp.where(chosen, spot(weight, p), weight_k)
            parts.append((radius_k, weight_k))
        tables[s] = [jnp.concatenate([p[n] for p in parts], 0) for n in range(2)]
        tables[s] += [row_x[s, n, :, :] for n in (2, 3, 4)]

    def spread(parts, size, dim, index):
        back = turn(parts[-1], -1, dim)
        ahead = turn(parts[1], 1, dim)
        inner = parts[0] + jnp.where(index == size - 1, 0.0, back) + jnp.where(index == 0, 0.0, ahead)
        outer = jnp.where(index == size - 1, back, jnp.where(index == 0, ahead, 0.0))
        return inner, outer

    own = []
    for l in range(levels):
        inner = {}
        for b in SHIFTS:
            parts = {a: deposit[a, b][l * cx : (l + 1) * cx] for a in SHIFTS}
            inner[b], _ = spread(parts, cx, 0, line)
            inner[b] = inner[b] + jnp.where(
                line == 0, arrive[l][0][b], jnp.where(line == cx - 1, arrive[l][1][b], 0.0)
            )
        kept, leaving = spread(inner, cy, 1, lane)
        own.append(kept)
        dep_out[l] = leaving
    deposits = []
    for t, dy in enumerate(ys):
        deposits.append(send(dep_out, dep_in.at[t], y_send.at[t, 1], y_recv.at[t, 1], (0, dy)))

    for n in range(5):
        face = pick_y((size_out, coal)[n][...]) if n < 2 else fixed_y[n - 2]
        edge[n : n + 1, :] = face + pick_c(0, tables[0][n]) + pick_c(1, tables[1][n])
    edges = []
    for t, dy in enumerate(ys):
        edges.append(send(edge, edge_in.at[t], y_send.at[t, 2], y_recv.at[t, 2], (0, dy)))

    for s in range(2):
        got = pick(tables[s], *hots[s])
        for n in range(5):
            rec_out[n, :, pl.ds(s * kx, kx)] = got[n]

    for copy in deposits:
        copy.wait_recv()
    for l in range(levels):
        if len(ys) == 1:
            total = own[l] + dep_in[0, l]
        else:
            total = own[l] + jnp.where(
                lane == 0, dep_in[0, l], jnp.where(lane == cy - 1, dep_in[1, l], 0.0)
            )
        moist_out[l] = moist_out[l] - VAPOUR_PER_SOURCE * total
        warm_out[l] = warm_out[l] + WARMING_FACTOR * total

    for copy in edges:
        copy.wait_recv()
    came = edge_in[0]
    if len(ys) == 2:
        came = jnp.where(jnp.broadcast_to(high, (8, width)), came, edge_in[1])
    for n in range(5):
        rec_out[n, :, pl.ds(2 * kx, width)] = came[n : n + 1, :]
    box_out[:, pl.ds(2 * kx, width)] = came[5:6, :].astype(jnp.int32)

    for copy in sends:
        copy.wait_send()


def publish(*refs):
    count = len(refs) // 2
    sems = refs[-1]
    copies = [
        pltpu.make_async_copy(refs[n], refs[count + n], sems.at[n]) for n in range(count)
    ]
    for copy in copies:
        copy.start()
    for copy in copies:
        copy.wait()


def per_device(nx, ny, moist, warm, size, mult, dry, east, north, perm, lx, ly, lc):
    levels, cx, cy = moist.shape
    sd = size.shape[0]
    kx, ky, kc = lx.shape[2], ly.shape[2], lc.shape[2]
    narr = 2 * kx + 2 * ky + 4 * kc
    width = 2 * ky + 4 * kc
    slots = sd * levels * cx
    flat = [x.reshape(slots, cy) for x in (size, mult, dry, east, north, perm)]
    f32, i32 = jnp.float32, jnp.int32
    any_space = pl.BlockSpec(memory_space=pl.ANY)
    vmem_space = pl.BlockSpec(memory_space=pltpu.VMEM)
    dma = pltpu.SemaphoreType.DMA
    shapes = (
        ((levels, cx, cy), f32),
        ((levels, cx, cy), f32),
        ((slots, cy), f32),
        ((slots, cy), f32),
        ((5, 1, narr), f32),
        ((1, narr), i32),
    )
    n_y = 1 if ny == 2 else 2
    outs = pl.pallas_call(
        functools.partial(body, (levels, cx, cy, sd, kx, ky, kc, nx, ny)),
        out_shape=tuple(pltpu.VMEM(*s) for s in shapes),
        in_specs=[any_space] * 11,
        out_specs=[vmem_space] * 6,
        scratch_shapes=[
            pltpu.VMEM((2, levels, cx, cy), f32),
            pltpu.VMEM((5, slots, cy), f32),
            pltpu.VMEM((slots, cy), i32),
            pltpu.VMEM((2, kx), i32),
            pltpu.VMEM((2, ky), i32),
            pltpu.VMEM((4, kc), i32),
            pltpu.VMEM((2, 2, cx, cy), f32),
            pltpu.VMEM((2, 2, cx, cy), f32),
            pltpu.VMEM((n_y, 2, levels, cx, cy), f32),
            pltpu.VMEM((2, n_y, 2, cx, cy), f32),
            pltpu.VMEM((2, 1, kx + 128), i32),
            pltpu.VMEM((2, 1, kx + 128), i32),
            pltpu.VMEM((2, 6, sd * levels, cy), f32),
            pltpu.VMEM((2, 6, sd * levels, cy), f32),
            pltpu.VMEM((levels, cx, cy), f32),
            pltpu.VMEM((n_y, levels, cx, cy), f32),
            pltpu.VMEM((8, width), f32),
            pltpu.VMEM((n_y, 8, width), f32),
            pltpu.VMEM((slots, cy), f32),
            pltpu.VMEM((slots, cy), f32),
            dma((11,)),
            dma((2, 3)), dma((2, 3)), dma((2, n_y)), dma((2, n_y)), dma((n_y, 3)), dma((n_y, 3)),
        ],
        compiler_params=pltpu.CompilerParams(collective_id=0, has_side_effects=True),
    )(moist, warm, *flat, lx, ly, lc)
    outs = pl.pallas_call(
        publish,
        out_shape=tuple(jax.ShapeDtypeStruct(*s) for s in shapes),
        in_specs=[vmem_space] * 6,
        out_specs=[any_space] * 6,
        scratch_shapes=[dma((6,))],
    )(*[pltpu.with_memory_space_constraint(x, pltpu.VMEM) for x in outs])
    return (
        outs[0], outs[1], outs[2].reshape(size.shape), outs[3].reshape(size.shape), outs[4], outs[5],
    )


def solution(mesh):
    cell, drop, lists = P(None, "gx", "gy"), P(None, None, "gx", "gy"), P("gx", None, "gy")
    return jax.shard_map(
        functools.partial(per_device, mesh.shape["gx"], mesh.shape["gy"]),
        mesh=mesh,
        in_specs=(cell,) * 2 + (drop,) * 6 + (lists,) * 3,
        out_specs=(cell, cell, drop, drop, cell, P("gx", "gy")),
        check_vma=False,
    )
```

profile of v0, /device:TPU:0, one launch (start us, length us, event | category | flops | bytes accessed | tf_op | source)
XLA Modules:
  0.0 13.4 jit_solution(17962105895572076871)
XLA Ops:
  0.6 12.0 %shard_map.154 = (f32[2,8,128]{2,1,0:T(8,128)S(1)}, f32[2,8,128]{2,1,0:T(8,128)S(1)}, f32[128,128]{1,0:T(8,128)S(1)}, f32[128,128]{1,0:T(8,128)S(1)}, f32[5,1,2176]{2,1,0:T(1,128)S(1)}, /*index=5*/s32[1,2176]{1,0:T(1,128)S(1)}) custom-call(f32[2,8,128]{2,1,0:T(8,128)} %moist_in.1, f32[2,8,128]{2,1,0:T(8,128)} %warm_in.1, f32[128,128]{1,0:T(8,128)} %bitcast.8, ...), custom_call_target="tpu_custom_call" | custom-call | tf_op jit(solution)/shard_map/pallas_call | solution.py:496
  12.6 0.7 %shard_map.155 = (f32[2,8,128]{2,1,0:T(8,128)}, f32[2,8,128]{2,1,0:T(8,128)}, f32[128,128]{1,0:T(8,128)}, f32[128,128]{1,0:T(8,128)}, f32[5,1,2176]{2,1,0:T(1,128)}, /*index=5*/s32[1,2176]{1,0:T(1,128)}) custom-call(f32[2,8,128]{2,1,0:T(8,128)S(1)} %get-tuple-element.18.refs_0_, f32[2,8,128]{2,1,0:T(8,128)S(1)} %get-tuple-element.19.refs_1_, ...), custom_call_target="tpu_custom_call" | custom-call | tf_op jit(solution)/shard_map/pallas_call | solution.py:527
where the time goes:
time: 13.6 us; the launch traced here: 13.4 us
  Pallas kernels  12.7 us (93%)
  between operations  0.64 us (5%)
    pallas_call x1, Pallas kernels, per_device(): pl.pallas_call(functools.partial(body, (levels, cx, cy, sd, kx, ky, kc, n...  12 us
    pallas_call x1, Pallas kernels, per_device(): pl.pallas_call(publish, out_shape=tuple((jax.ShapeDtypeStruct(*s) for s i...  0.73 us

commit v1 on v0

v1 whole, which is shorter than its diff:
```python
import functools
import math

import jax
import jax.numpy as jnp
from jax import lax
from jax.experimental import pallas as pl
from jax.experimental.pallas import tpu as pltpu
from jax.sharding import PartitionSpec as P

NEWTON = 4
MIX_HORIZONTAL = 0.2
MIX_VERTICAL = 0.05
EXCESS_FACTOR = 4.2222
CURVATURE = 0.0012
KAPPA_SOLUTE = 0.6
GROWTH_STEP = 200.0
COLLIDE_RATE = 4e-07
VAPOUR_PER_SOURCE = 0.001
WARMING_FACTOR = 0.00249
LOG2E = math.log2(math.e)

MESH = pl.DeviceIdType.MESH
SHIFTS = (-1, 0, 1)
SIDES = (1, -1)
MOVES = (1, -1)


def div(x, n):
    return lax.shift_right_arithmetic(x, jnp.int32(n.bit_length() - 1))


def mod(x, n):
    return lax.bitwise_and(x, jnp.int32(n - 1))


def iota(shape, dim):
    return lax.broadcasted_iota(jnp.int32, shape, dim)


def turn(x, shift, dim):
    shift %= x.shape[dim]
    return pltpu.roll(x, shift, dim) if shift else x


def take(x, index, dim):
    return jnp.take_along_axis(x, index, axis=dim)


def kernel_weights(offset):
    return {
        -1: jnp.maximum(0.5 - offset, 0.0),
        0: 1.0 - jnp.abs(offset - 0.5),
        1: jnp.maximum(offset - 0.5, 0.0),
    }


def prepare(radius, dry):
    inverse = 1.0 / radius
    square = inverse * inverse
    lowest = dry * dry
    strength = (1.5 * GROWTH_STEP * KAPPA_SOLUTE) * (lowest * dry)
    pull = strength * (square * inverse)
    area = radius * radius
    return (
        area - (GROWTH_STEP * CURVATURE) * inverse,
        (5.0 / 3.0) * pull,
        1.0 / (1.0 + pull * square),
        strength,
        lowest,
        area * radius,
    )


def settle(level, top, inverse_slope, strength, lowest):
    wetted = jnp.maximum((level + top) * inverse_slope, lowest)
    for sweep in range(NEWTON - 1):
        inverse_root = lax.rsqrt(wetted)
        square = inverse_root * inverse_root
        pull = strength * (square * inverse_root)
        wetted = jnp.maximum((level + (5.0 / 3.0) * pull) / (1.0 + pull * square), lowest)
    root = wetted * lax.rsqrt(wetted)
    return root, wetted * root


def differences(field):
    near = {(a, b): turn(turn(field, -b, 1), -a, 0) for a in SHIFTS for b in SHIFTS}
    terms = {(0, 0): field}
    for s in SIDES:
        terms[s, 0] = near[s, 0] - field
        terms[0, s] = near[0, s] - field
    for a in SIDES:
        for b in SIDES:
            terms[a, b] = near[a, b] - near[a, 0] - terms[0, b]
    return terms


def interpolate(terms, east, north, reach_x, reach_y):
    right, up = east > 0.5, north > 0.5
    slope_x = jnp.where(right, terms[1, 0], terms[-1, 0])
    slope_y = jnp.where(up, terms[0, 1], terms[0, -1])
    twist = jnp.where(
        right, jnp.where(up, terms[1, 1], terms[1, -1]), jnp.where(up, terms[-1, 1], terms[-1, -1])
    )
    return terms[0, 0] + reach_x * slope_x + reach_y * (slope_y + reach_x * twist)


def match(weight, other, first):
    big = (weight > other) | ((weight == other) & first)
    rate = (-COLLIDE_RATE * LOG2E) * jnp.where(big, weight, other)
    return rate, jnp.where(big, other, 0.0)


def collide(radius, cube, other, rate, eaten):
    total = radius + other
    chance = 1.0 - jnp.exp2(rate * (total * total) * (total * jnp.abs(radius - other)))
    volume = cube + chance * (other * other * other)
    merged = jnp.exp2(jnp.log(volume) * (LOG2E / 3.0))
    return jnp.where(eaten > 0.0, radius, merged), chance * eaten


def body(
    sizes,
    moist_in, warm_in, size_in, mult_in, dry_in, east_in, north_in, perm_in,
    lx_in, ly_in, lc_in,
    moist_out, warm_out, size_out, mult_out, rec_out, box_out,
    state, drops, perm, lx, ly, lc,
    state_pack, state_x, state_y, diag_pack, diag_in,
    list_pack, list_x, list_c, row_pack, row_x, corner_pack, corner_in,
    dep_out, dep_in, edge, edge_in, mask, coal,
    ready, share, bits, near, late_x,
    in_sem, x_send, x_recv, c_send, c_recv, y_send, y_recv,
):
    levels, cx, cy, sd, kx, ky, kc, nx, ny = sizes
    me_x = lax.axis_index("gx")
    me_y = lax.axis_index("gy")
    ys = (1,) if ny == 2 else (1, -1)
    half = cx // 2
    rows = sd * levels
    block = cx * cy
    tall = levels * cx
    deep = kx // cy

    def at(d):
        return (lax.rem(me_x + d[0] + nx, nx), lax.rem(me_y + d[1] + ny, ny))

    loads = []

    def load(source, target):
        copy = pltpu.make_async_copy(source, target, in_sem.at[len(loads)])
        copy.start()
        loads.append(copy)

    load(moist_in, state.at[0])
    load(warm_in, state.at[1])
    for n, source in enumerate((size_in, mult_in, dry_in, east_in, north_in)):
        load(source, drops.at[n])
    load(perm_in, perm)
    load(lx_in.at[0], lx)
    load(ly_in.at[0], ly)
    load(lc_in.at[0], lc)

    friends = [(dx, 0) for dx in MOVES] + [(dx, dy) for dx in MOVES for dy in ys] + [(0, dy) for dy in ys]
    barrier = pltpu.get_barrier_semaphore()
    for d in friends:
        pl.semaphore_signal(barrier, inc=1, device_id=at(d), device_id_type=MESH)

    sends = []

    def send(source, target, s_sem, r_sem, d):
        copy = pltpu.make_async_remote_copy(
            src_ref=source, dst_ref=target, send_sem=s_sem, recv_sem=r_sem,
            device_id=at(d), device_id_type=MESH,
        )
        copy.start()
        sends.append(copy)
        return copy

    line = iota((cx, cy), 0)
    lane = iota((cx, cy), 1)
    low_half = line < half
    middle = (lane >= cy // 4) & (lane < 3 * cy // 4)

    loads[0].wait()
    loads[1].wait()
    for s in range(2):
        tiles = []
        for f in range(2):
            first, second = state[f, 0], turn(state[f, 1], half, 0)
            tiles.append(jnp.where(low_half, second, first) if s == 0 else jnp.where(low_half, first, second))
            state_pack[s, f] = tiles[f]
        diag_pack[s] = jnp.where(middle, turn(tiles[1], cy // 2, 1), tiles[0])

    pl.semaphore_wait(barrier, len(friends))

    early = []
    for s, dx in enumerate(MOVES):
        early.append(send(state_pack.at[s], state_x.at[s], x_send.at[s, 0], x_recv.at[s, 0], (dx, 0)))
    for s, dx in enumerate(MOVES):
        for t, dy in enumerate(ys):
            early.append(
                send(diag_pack.at[s], diag_in.at[s, t], c_send.at[s, t, 0], c_recv.at[s, t, 0], (dx, dy))
            )
    for t, dy in enumerate(ys):
        early.append(send(state, state_y.at[t], y_send.at[t, 0], y_recv.at[t, 0], (0, dy)))

    for copy in loads[2:]:
        copy.wait()
    late = []
    for s, (dx, side) in enumerate(zip(MOVES, (cx - 1, 0))):
        for l in range(levels):
            picked = pl.ds(l * cx + side, sd, stride=tall)
            for n in range(5):
                row_pack[s, n, pl.ds(l * sd, sd), :] = drops[n, picked, :]
            row_pack[s, 5, pl.ds(l * sd, sd), :] = perm[picked, :].astype(jnp.float32)
        late.append(send(row_pack.at[s], row_x.at[s], x_send.at[s, 2], x_recv.at[s, 2], (dx, 0)))
    for s, dx in enumerate(MOVES):
        for c in range(deep):
            list_pack[s, c : c + 1, :] = lx[s : s + 1, c * cy : (c + 1) * cy]
        late.append(send(list_pack.at[s], list_x.at[s], x_send.at[s, 1], x_recv.at[s, 1], (dx, 0)))
    for s, dx in enumerate(MOVES):
        tile = None
        for n in range(6):
            for l in range(levels):
                spot = 8 * n + 4 * s + 2 * l
                moved = turn(row_pack[s, n, pl.ds(l * sd, sd), :], spot + 1, 1)
                tile = moved if tile is None else jnp.where((lane >= spot) & (lane < spot + 2), moved, tile)
        corner_pack[s] = tile
        for t, dy in enumerate(ys):
            late.append(
                send(corner_pack.at[s], corner_in.at[s, t], c_send.at[s, t, 1], c_recv.at[s, t, 1], (dx, dy))
            )
            late.append(send(lc, list_c.at[s, t], c_send.at[s, t, 2], c_recv.at[s, t, 2], (dx, dy)))

    order = [perm[k * tall : (k + 1) * tall, :] for k in range(sd)]
    for m in range(sd):
        part = pl.ds(m * tall, tall)
        weight = drops[1, part, :]
        partner = jnp.zeros((tall, cy), jnp.int32)
        first = jnp.zeros((tall, cy), jnp.int32)
        for p in range(sd):
            mine = order[p] == m
            partner = jnp.where(mine, order[p ^ 1], partner)
            if p % 2 == 0:
                first = jnp.where(mine, 1, first)
        other = drops[1, pl.ds(0, tall), :]
        for k in range(1, sd):
            other = jnp.where(partner == k, drops[1, pl.ds(k * tall, tall), :], other)
        rate, eaten = match(weight, other, first > 0)
        for n in range(3):
            bits[n, part, :] = mod(lax.shift_right_logical(partner, jnp.int32(n)), 2)
        for n, value in enumerate(prepare(drops[0, part, :], drops[2, part, :])):
            ready[n, part, :] = value
        east, north = drops[3, part, :], drops[4, part, :]
        ready[6, part, :] = jnp.abs(east - 0.5)
        ready[7, part, :] = jnp.abs(north - 0.5)
        ready[8, part, :] = rate
        ready[9, part, :] = eaten
        wx, wy = kernel_weights(east), kernel_weights(north)
        for a in SHIFTS:
            along = wx[a] * weight
            for b in SHIFTS:
                share[3 * a + b + 4, part, :] = wy[b] * along

    mask[...] = jnp.ones_like(mask)
    for r, side in enumerate((cx - 1, 0)):
        slots = lx[r : r + 1, :]
        hot_row = iota((rows, kx), 0) == div(slots, block)
        hot_lane = jnp.where(iota((cy, kx), 0) == mod(slots, cy), 1.0, 0.0).astype(jnp.bfloat16)
        named = lax.dot_general(
            jnp.where(hot_row, 1.0, 0.0).astype(jnp.bfloat16), hot_lane,
            (((1,), (1,)), ((), ())), preferred_element_type=jnp.float32,
        )
        mask[pl.ds(side, rows, stride=cx), :] = 1.0 - named

    width = 2 * ky + 4 * kc
    lane_e = iota((1, width), 1)
    high = (lane_e < ky) | ((lane_e >= 2 * ky) & (lane_e < 2 * ky + 2 * kc))
    high_all = jnp.broadcast_to(high, (rows * cx, width))
    slots = jnp.concatenate(
        [ly[0:1, :], ly[1:2, :], lc[0:1, :], lc[2:3, :], lc[1:2, :], lc[3:4, :]], 1
    )
    named_e = iota((rows * cx, width), 0) == div(slots, cy)
    hot_e = jnp.where(named_e, 1.0, 0.0)
    left_high = jnp.max(jnp.where(high_all, hot_e, 0.0), 1, keepdims=True)
    left_low = jnp.max(jnp.where(high_all, 0.0, hot_e), 1, keepdims=True)
    lane_all = iota((rows * cx, cy), 1)
    mask[...] = mask[...] * (
        1.0 - jnp.where(lane_all == cy - 1, left_high, jnp.where(lane_all == 0, left_low, 0.0))
    )

    face = lane_e < 2 * ky
    face_pile = jnp.broadcast_to(jnp.where(face, div(slots, block), -1), (cx, width))
    face_line = line == mod(div(slots, cy), cx)
    face_lane = jnp.broadcast_to(jnp.where(high, cy - 1, 0), (cx, width))

    def pick_y(ref):
        got = jnp.zeros((cx, width), jnp.float32)
        for n in range(rows):
            got = jnp.where(face_pile == n, take(ref[pl.ds(n * cx, cx), :], face_lane, 1), got)
        return jnp.sum(jnp.where(face_line, got, 0.0), 0, keepdims=True)

    def land(slots, move_x, move_y):
        level = mod(div(slots, block), levels)
        i = mod(mod(div(slots, cy), cx) + move_x, cx)
        target = (level * cx + i) * cy + mod(mod(slots, cy) + move_y, cy)
        return jnp.where(slots >= 0, target, -1)

    for n in (2, 3, 4):
        edge[n : n + 1, :] = pick_y(drops.at[n])
    edge[5:6, :] = land(slots, 0, jnp.where(high, 1, -1)).astype(jnp.float32)
    edge[6:8, :] = jnp.zeros((2, width), jnp.float32)

    for copy in early:
        copy.wait_recv()

    def blend(parts, pick_second):
        return parts[0] if len(parts) == 1 else jnp.where(pick_second, parts[1], parts[0])

    left_lanes = lane < cy // 2
    fields = []
    for f in range(2):
        fields.append([])
        for l in range(levels):
            def beyond(up, down):
                return jnp.where(low_half, turn(down, half * l, 0), turn(up, half * l, 0))

            across = beyond(state_x[0, f], state_x[1, f])
            tiles = [[turn(diag_in[s, t], f * (cy // 2), 1) for s in range(2)] for t in range(len(ys))]
            far = blend([beyond(*pair) for pair in tiles], left_lanes)
            side_y = blend([state_y[t, f, l] for t in range(len(ys))], left_lanes)
            own_half = jnp.concatenate([state[f, l], across], 0)
            fields[f].append(jnp.concatenate([own_half, jnp.concatenate([side_y, far], 0)], 1))
    mixed = []
    for f in range(2):
        mixed.append([])
        for l in range(levels):
            centre = fields[f][l]
            around = turn(centre, -1, 0) + turn(centre, 1, 0) + turn(centre, -1, 1) + turn(centre, 1, 1)
            stacked = fields[f][min(l + 1, levels - 1)] + fields[f][max(l - 1, 0)]
            mixed[f].append(
                (1.0 - 4.0 * MIX_HORIZONTAL - 2.0 * MIX_VERTICAL) * centre
                + MIX_HORIZONTAL * around + MIX_VERTICAL * stacked
            )
    keys = [(a, b) for a in SHIFTS for b in SHIFTS]
    terms = []
    for l in range(levels):
        vapour, warmth = mixed[0][l], mixed[1][l]
        decay = jnp.exp2((-17.27 * LOG2E) * (warmth - 273.15) / (warmth - 35.86))
        terms.append(differences((GROWTH_STEP / EXCESS_FACTOR) * (vapour * decay) - GROWTH_STEP))
        moist_out[l] = vapour[:cx, :cy]
        warm_out[l] = warmth[:cx, :cy]
    window = {key: jnp.concatenate([t[key][:cx, :cy] for t in terms], 0) for key in keys}

    grown = []
    cubes = []
    deposit = {}
    for k in range(sd):
        part = pl.ds(k * tall, tall)
        base, top, inverse_slope, strength, lowest, cube = (ready[n, part, :] for n in range(6))
        level = base + interpolate(
            window, drops[3, part, :], drops[4, part, :], ready[6, part, :], ready[7, part, :]
        )
        root, volume = settle(level, top, inverse_slope, strength, lowest)
        gain = volume - cube
        for a, b in keys:
            term = share[3 * a + b + 4, part, :] * gain
            deposit[a, b] = term if k == 0 else deposit[a, b] + term
        grown.append(root)
        cubes.append(volume)

    def spread(parts, dim, index):
        size = parts[0].shape[dim]
        back = turn(parts[-1], -1, dim)
        ahead = turn(parts[1], 1, dim)
        inner = parts[0] + jnp.where(index == size - 1, 0.0, back) + jnp.where(index == 0, 0.0, ahead)
        outer = jnp.where(index == size - 1, back, jnp.where(index == 0, ahead, 0.0))
        return inner, outer

    own = []
    for l in range(levels):
        inner = {}
        for b in SHIFTS:
            inner[b], _ = spread({a: deposit[a, b][l * cx : (l + 1) * cx] for a in SHIFTS}, 0, line)
        kept, leaving = spread(inner, 1, lane)
        own.append(kept)
        dep_out[l] = leaving
    deposits = []
    for t, dy in enumerate(ys):
        deposits.append(send(dep_out, dep_in.at[t], y_send.at[t, 1], y_recv.at[t, 1], (0, dy)))

    for m in range(sd):
        part = pl.ds(m * tall, tall)
        found = grown
        for n in range(3):
            odd = bits[n, part, :] > 0
            found = [jnp.where(odd, found[2 * i + 1], found[2 * i]) for i in range(len(found) // 2)]
        radius, lost = collide(grown[m], cubes[m], found[0], ready[8, part, :], ready[9, part, :])
        weight = drops[1, part, :] - lost
        size_out[part, :] = radius
        coal[part, :] = weight
        mult_out[part, :] = mask[part, :] * weight

    edge[0:1, :] = pick_y(size_out)
    edge[1:2, :] = pick_y(coal)
    edges = []
    for t, dy in enumerate(ys):
        edges.append(send(edge, edge_in.at[t], y_send.at[t, 2], y_recv.at[t, 2], (0, dy)))

    for l in range(levels):
        for n, key in enumerate(keys):
            near[l, n] = terms[l][key][cx:, :cy]
    corner_window = {}
    for key in keys:
        built = None
        for s, home in enumerate((2 * cx - 1, cx)):
            for l in range(levels):
                spot = 4 * s + 2 * l
                moved = turn(jnp.broadcast_to(terms[l][key][home : home + 1, cy:], (sd, cy)), spot + 1, 1)
                built = moved if built is None else jnp.where(lane >= spot, moved, built)
        corner_window[key] = built

    for copy in late:
        copy.wait_recv()

    def pair_up(weight, turns):
        seat = iota((sd, cy), 0)
        rank = jnp.zeros((sd, cy), jnp.int32)
        for p in range(1, sd):
            rank = jnp.where(jnp.broadcast_to(turns[p : p + 1], (sd, cy)) == seat, p, rank)
        partner = take(turns, rank ^ 1, 0)
        return partner, match(weight, take(weight, partner, 0), mod(rank, 2) == 0)

    def finish(radius, weight, dry, east, north, turns, around):
        base, top, inverse_slope, strength, lowest, cube = prepare(radius, dry)
        level = base + interpolate(around, east, north, jnp.abs(east - 0.5), jnp.abs(north - 0.5))
        root, volume = settle(level, top, inverse_slope, strength, lowest)
        partner, (rate, eaten) = pair_up(weight, turns.astype(jnp.int32))
        after, lost = collide(root, volume, take(root, partner, 0), rate, eaten)
        return weight * (volume - cube), after, weight - lost

    arrive = [[None, None] for l in range(levels)]
    for s in range(2):
        home = cx - 1 if s == 0 else 0
        for l in range(levels):
            span = pl.ds(l * sd, sd)
            values = [row_x[s, n, span, :] for n in range(6)]
            around = {
                key: jnp.broadcast_to(near[l, n, home : home + 1, :], (sd, cy)) for n, key in enumerate(keys)
            }
            condensed, radius, weight = finish(*values, around)
            late_x[s, 0, span, :] = radius
            late_x[s, 1, span, :] = weight
            wx, wy = kernel_weights(values[3]), kernel_weights(values[4])
            along = wx[MOVES[s]] * condensed
            moved = {b: jnp.sum(wy[b] * along, 0, keepdims=True) for b in SHIFTS}
            arrive[l][s], _ = spread(moved, 1, lane[0:1])

    tile = [blend([corner_in[s, t] for t in range(len(ys))], mod(lane, 2) == 1) for s in range(2)]
    tile = jnp.where(mod(lane, 8) < 4, tile[0], tile[1])
    values = [turn(tile, -8 * n, 1) for n in range(6)]
    condensed, corner_radius, corner_weight = finish(*values, corner_window)
    wx, wy = kernel_weights(values[3]), kernel_weights(values[4])
    drop_x = jnp.where(mod(lane, 8) < 4, wx[1], wx[-1])
    drop_y = jnp.where(mod(lane, 2) == 0, wy[1], wy[-1])
    fallen = jnp.sum(drop_x * drop_y * condensed, 0, keepdims=True)
    for l in range(levels):
        for s in range(2):
            spot = 4 * s + 2 * l
            added = arrive[l][s] + jnp.where(
                lane[0:1] == 0, turn(fallen, -spot, 1),
                jnp.where(lane[0:1] == cy - 1, turn(fallen, cy - 2 - spot, 1), 0.0),
            )
            own[l] = own[l] + jnp.where(line == (0 if s == 0 else cx - 1), added, 0.0)

    for s, dx in enumerate(MOVES):
        slots = list_x[s]
        level = mod(div(slots, block), levels)
        row = jnp.where(slots >= 0, level * sd + div(slots, block * levels), -1)
        column = mod(slots, cy)
        for n in range(5):
            got = jnp.zeros((deep, cy), jnp.float32)
            for r in range(rows):
                source = late_x[s, n, r : r + 1, :] if n < 2 else row_x[s, n, r : r + 1, :]
                got = jnp.where(row == r, take(jnp.broadcast_to(source, (deep, cy)), column, 1), got)
            rec_out[n, :, pl.ds(s * kx, kx)] = got.reshape(1, kx)
        box_out[:, pl.ds(s * kx, kx)] = land(slots, dx, 0).reshape(1, kx)

    blank = jnp.full((1, 2 * ky), -1, jnp.int32)
    slots = jnp.concatenate(
        [blank] + [
            list_c[s, d if len(ys) == 2 else 0, 2 * s + d : 2 * s + d + 1, :] for d in range(2) for s in range(2)
        ],
        1,
    )
    which = div(lane_e - 2 * ky, kc)
    minus_x, minus_y = mod(which, 2), div(which, 2)
    level = mod(div(slots, block), levels)
    spot = jnp.broadcast_to(jnp.where(slots >= 0, 4 * minus_x + 2 * level + minus_y, 0), (sd, width))
    seat = jnp.where(slots >= 0, div(slots, block * levels), -1)
    corner_box = land(slots, 1 - 2 * minus_x, 1 - 2 * minus_y)
    corner_rec = [
        jnp.sum(jnp.where(iota((sd, width), 0) == seat, take(value, spot, 1), 0.0), 0, keepdims=True)
        for value in (corner_radius, corner_weight, values[2], values[3], values[4])
    ]

    for copy in deposits:
        copy.wait_recv()
    for l in range(levels):
        if len(ys) == 1:
            total = own[l] + dep_in[0, l]
        else:
            total = own[l] + jnp.where(
                lane == 0, dep_in[0, l], jnp.where(lane == cy - 1, dep_in[1, l], 0.0)
            )
        moist_out[l] = moist_out[l] - VAPOUR_PER_SOURCE * total
        warm_out[l] = warm_out[l] + WARMING_FACTOR * total

    for copy in edges:
        copy.wait_recv()
    came = blend([edge_in[t] for t in range(len(ys))], jnp.broadcast_to(lane_e >= ky, (8, width)))
    for n in range(5):
        rec_out[n, :, pl.ds(2 * kx, width)] = jnp.where(face, came[n : n + 1, :], corner_rec[n])
    box_out[:, pl.ds(2 * kx, width)] = jnp.where(face, came[5:6, :].astype(jnp.int32), corner_box)

    for copy in sends:
        copy.wait_send()


def publish(*refs):
    count = len(refs) // 2
    sems = refs[-1]
    copies = [
        pltpu.make_async_copy(refs[n], refs[count + n], sems.at[n]) for n in range(count)
    ]
    for copy in copies:
        copy.start()
    for copy in copies:
        copy.wait()


def per_device(nx, ny, moist, warm, size, mult, dry, east, north, perm, lx, ly, lc):
    levels, cx, cy = moist.shape
    sd = size.shape[0]
    kx, ky, kc = lx.shape[2], ly.shape[2], lc.shape[2]
    narr = 2 * kx + 2 * ky + 4 * kc
    width = 2 * ky + 4 * kc
    slots = sd * levels * cx
    flat = [x.reshape(slots, cy) for x in (size, mult, dry, east, north, perm)]
    f32, i32 = jnp.float32, jnp.int32
    any_space = pl.BlockSpec(memory_space=pl.ANY)
    vmem_space = pl.BlockSpec(memory_space=pltpu.VMEM)
    dma = pltpu.SemaphoreType.DMA
    shapes = (
        ((levels, cx, cy), f32),
        ((levels, cx, cy), f32),
        ((slots, cy), f32),
        ((slots, cy), f32),
        ((5, 1, narr), f32),
        ((1, narr), i32),
    )
    n_y = 1 if ny == 2 else 2
    outs = pl.pallas_call(
        functools.partial(body, (levels, cx, cy, sd, kx, ky, kc, nx, ny)),
        out_shape=tuple(pltpu.VMEM(*s) for s in shapes),
        in_specs=[any_space] * 11,
        out_specs=[vmem_space] * 6,
        scratch_shapes=[
            pltpu.VMEM((2, levels, cx, cy), f32),
            pltpu.VMEM((5, slots, cy), f32),
            pltpu.VMEM((slots, cy), i32),
            pltpu.VMEM((2, kx), i32),
            pltpu.VMEM((2, ky), i32),
            pltpu.VMEM((4, kc), i32),
            pltpu.VMEM((2, 2, cx, cy), f32),
            pltpu.VMEM((2, 2, cx, cy), f32),
            pltpu.VMEM((n_y, 2, levels, cx, cy), f32),
            pltpu.VMEM((2, cx, cy), f32),
            pltpu.VMEM((2, n_y, cx, cy), f32),
            pltpu.VMEM((2, kx // cy, cy), i32),
            pltpu.VMEM((2, kx // cy, cy), i32),
            pltpu.VMEM((2, n_y, 4, kc), i32),
            pltpu.VMEM((2, 6, sd * levels, cy), f32),
            pltpu.VMEM((2, 6, sd * levels, cy), f32),
            pltpu.VMEM((2, sd, cy), f32),
            pltpu.VMEM((2, n_y, sd, cy), f32),
            pltpu.VMEM((levels, cx, cy), f32),
            pltpu.VMEM((n_y, levels, cx, cy), f32),
            pltpu.VMEM((8, width), f32),
            pltpu.VMEM((n_y, 8, width), f32),
            pltpu.VMEM((slots, cy), f32),
            pltpu.VMEM((slots, cy), f32),
            pltpu.VMEM((10, slots, cy), f32),
            pltpu.VMEM((9, slots, cy), f32),
            pltpu.VMEM((3, slots, cy), i32),
            pltpu.VMEM((levels, 9, cx, cy), f32),
            pltpu.VMEM((2, 2, sd * levels, cy), f32),
            dma((11,)),
            dma((2, 3)), dma((2, 3)), dma((2, n_y, 3)), dma((2, n_y, 3)), dma((n_y, 3)), dma((n_y, 3)),
        ],
        compiler_params=pltpu.CompilerParams(collective_id=0, has_side_effects=True),
    )(moist, warm, *flat, lx, ly, lc)
    outs = pl.pallas_call(
        publish,
        out_shape=tuple(jax.ShapeDtypeStruct(*s) for s in shapes),
        in_specs=[vmem_space] * 6,
        out_specs=[any_space] * 6,
        scratch_shapes=[dma((6,))],
    )(*[pltpu.with_memory_space_constraint(x, pltpu.VMEM) for x in outs])
    return (
        outs[0], outs[1], outs[2].reshape(size.shape), outs[3].reshape(size.shape), outs[4], outs[5],
    )


def solution(mesh):
    cell, drop, lists = P(None, "gx", "gy"), P(None, None, "gx", "gy"), P("gx", None, "gy")
    return jax.shard_map(
        functools.partial(per_device, mesh.shape["gx"], mesh.shape["gy"]),
        mesh=mesh,
        in_specs=(cell,) * 2 + (drop,) * 6 + (lists,) * 3,
        out_specs=(cell, cell, drop, drop, cell, P("gx", "gy")),
        check_vma=False,
    )
```

time: 13.6 us -> 12.8 us (0.941)
  Pallas kernels: 12.7 us -> 12 us
    pallas_call x1, Pallas kernels: 12 us -> 11.2 us  [per_device(): pl.pallas_call(functools.partial(body, (levels, cx, cy, sd, kx, ky, kc, n...]
where the time goes in v1:
time: 12.8 us; the launch traced here: 12.6 us
  Pallas kernels  12 us (94%)
  between operations  0.64 us (5%)
    pallas_call x1, Pallas kernels, per_device(): pl.pallas_call(functools.partial(body, (levels, cx, cy, sd, kx, ky, kc, n...  11.2 us
    pallas_call x1, Pallas kernels, per_device(): pl.pallas_call(publish, out_shape=tuple((jax.ShapeDtypeStruct(*s) for s i...  0.73 us

profile of v1, /device:TPU:0, one launch (start us, length us, event | category | flops | bytes accessed | tf_op | source)
XLA Modules:
  0.0 12.6 jit_solution(1841550474134790783)
XLA Ops:
  0.6 11.2 %shard_map.154 = (f32[2,8,128]{2,1,0:T(8,128)S(1)}, f32[2,8,128]{2,1,0:T(8,128)S(1)}, f32[128,128]{1,0:T(8,128)S(1)}, f32[128,128]{1,0:T(8,128)S(1)}, f32[5,1,2176]{2,1,0:T(1,128)S(1)}, /*index=5*/s32[1,2176]{1,0:T(1,128)S(1)}) custom-call(f32[2,8,128]{2,1,0:T(8,128)} %moist_in.1, f32[2,8,128]{2,1,0:T(8,128)} %warm_in.1, f32[128,128]{1,0:T(8,128)} %bitcast.8, ...), custom_call_target="tpu_custom_call" | custom-call | tf_op jit(solution)/shard_map/pallas_call | solution.py:563
  11.9 0.7 %shard_map.155 = (f32[2,8,128]{2,1,0:T(8,128)}, f32[2,8,128]{2,1,0:T(8,128)}, f32[128,128]{1,0:T(8,128)}, f32[128,128]{1,0:T(8,128)}, f32[5,1,2176]{2,1,0:T(1,128)}, /*index=5*/s32[1,2176]{1,0:T(1,128)}) custom-call(f32[2,8,128]{2,1,0:T(8,128)S(1)} %get-tuple-element.18.refs_0_, f32[2,8,128]{2,1,0:T(8,128)S(1)} %get-tuple-element.19.refs_1_, ...), custom_call_target="tpu_custom_call" | custom-call | tf_op jit(solution)/shard_map/pallas_call | solution.py:603

commit v2 on v1

v2 whole, which is shorter than its diff:
```python
import functools
import math

import jax
import jax.numpy as jnp
from jax import lax
from jax.experimental import pallas as pl
from jax.experimental.pallas import tpu as pltpu
from jax.sharding import PartitionSpec as P

NEWTON = 4
MIX_HORIZONTAL = 0.2
MIX_VERTICAL = 0.05
EXCESS_FACTOR = 4.2222
CURVATURE = 0.0012
KAPPA_SOLUTE = 0.6
GROWTH_STEP = 200.0
COLLIDE_RATE = 4e-07
VAPOUR_PER_SOURCE = 0.001
WARMING_FACTOR = 0.00249
LOG2E = math.log2(math.e)

MESH = pl.DeviceIdType.MESH
SHIFTS = (-1, 0, 1)
SIDES = (1, -1)
MOVES = (1, -1)


def div(x, n):
    return lax.shift_right_arithmetic(x, jnp.int32(n.bit_length() - 1))


def mod(x, n):
    return lax.bitwise_and(x, jnp.int32(n - 1))


def iota(shape, dim):
    return lax.broadcasted_iota(jnp.int32, shape, dim)


def turn(x, shift, dim):
    shift %= x.shape[dim]
    return pltpu.roll(x, shift, dim) if shift else x


def take(x, index, dim):
    return jnp.take_along_axis(x, index, axis=dim)


def kernel_weights(offset):
    return {
        -1: jnp.maximum(0.5 - offset, 0.0),
        0: 1.0 - jnp.abs(offset - 0.5),
        1: jnp.maximum(offset - 0.5, 0.0),
    }


def prepare(radius, dry):
    inverse = 1.0 / radius
    square = inverse * inverse
    lowest = dry * dry
    strength = (1.5 * GROWTH_STEP * KAPPA_SOLUTE) * (lowest * dry)
    pull = strength * (square * inverse)
    area = radius * radius
    return (
        area - (GROWTH_STEP * CURVATURE) * inverse,
        (5.0 / 3.0) * pull,
        1.0 / (1.0 + pull * square),
        strength,
        lowest,
        area * radius,
    )


def settle(level, top, inverse_slope, strength, lowest):
    wetted = jnp.maximum((level + top) * inverse_slope, lowest)
    for sweep in range(NEWTON - 1):
        inverse_root = lax.rsqrt(wetted)
        square = inverse_root * inverse_root
        pull = strength * (square * inverse_root)
        wetted = jnp.maximum((level + (5.0 / 3.0) * pull) / (1.0 + pull * square), lowest)
    root = wetted * lax.rsqrt(wetted)
    return root, wetted * root


def differences(near):
    centre = near[0, 0]
    terms = {(0, 0): centre}
    for s in SIDES:
        terms[s, 0] = near[s, 0] - centre
        terms[0, s] = near[0, s] - centre
    for a in SIDES:
        for b in SIDES:
            terms[a, b] = near[a, b] - near[a, 0] - terms[0, b]
    return terms


def interpolate(terms, east, north, reach_x, reach_y):
    right, up = east > 0.5, north > 0.5
    slope_x = jnp.where(right, terms[1, 0], terms[-1, 0])
    slope_y = jnp.where(up, terms[0, 1], terms[0, -1])
    twist = jnp.where(
        right, jnp.where(up, terms[1, 1], terms[1, -1]), jnp.where(up, terms[-1, 1], terms[-1, -1])
    )
    return terms[0, 0] + reach_x * slope_x + reach_y * (slope_y + reach_x * twist)


def match(weight, other, first):
    big = (weight > other) | ((weight == other) & first)
    rate = (-COLLIDE_RATE * LOG2E) * jnp.where(big, weight, other)
    return rate, jnp.where(big, other, 0.0)


def collide(radius, cube, other, rate, eaten):
    total = radius + other
    chance = 1.0 - jnp.exp2(rate * (total * total) * (total * jnp.abs(radius - other)))
    volume = cube + chance * (other * other * other)
    merged = jnp.exp2(jnp.log(volume) * (LOG2E / 3.0))
    return jnp.where(eaten > 0.0, radius, merged), chance * eaten


def spread(parts, dim, index):
    size = parts[0].shape[dim]
    back, ahead = turn(parts[-1], -1, dim), turn(parts[1], 1, dim)
    return parts[0] + jnp.where(index == size - 1, 0.0, back) + jnp.where(index == 0, 0.0, ahead)


def body(
    sizes,
    moist_in, warm_in, size_in, mult_in, dry_in, east_in, north_in, perm_in,
    lx_in, ly_in, lc_in,
    moist_out, warm_out, size_out, mult_out, rec_out, box_out,
    state, drops, perm, lx, ly, lc,
    state_pack, state_x, state_y, diag_pack, diag_in,
    list_pack, list_x, row_pack, row_x, corner_pack, corner_in, col_pack, col_in,
    mask, ready, share, bits, near, late_x,
    in_sem, send_sem, recv_sem,
):
    levels, cx, cy, sd, kx, ky, kc, nx, ny = sizes
    me_x = lax.axis_index("gx")
    me_y = lax.axis_index("gy")
    ys = (1,) if ny == 2 else (1, -1)
    half = cx // 2
    rows = sd * levels
    slots_all = rows * cx
    block = cx * cy
    tall = levels * cx
    deep = kx // cy
    note = cy // 2

    def at(d):
        return (lax.rem(me_x + d[0] + nx, nx), lax.rem(me_y + d[1] + ny, ny))

    for n, source in enumerate((moist_in, warm_in)):
        pltpu.make_async_copy(source, state.at[n], in_sem.at[0]).start()
    for n, source in enumerate((size_in, mult_in, dry_in, east_in, north_in)):
        pltpu.make_async_copy(source, drops.at[n], in_sem.at[1]).start()
    pltpu.make_async_copy(perm_in, perm, in_sem.at[1]).start()
    lists = [
        pltpu.make_async_copy(source.at[0], target, in_sem.at[2 + n])
        for n, (source, target) in enumerate(((lx_in, lx), (ly_in, ly), (lc_in, lc)))
    ]
    for copy in lists:
        copy.start()

    friends = [(dx, 0) for dx in MOVES] + [(dx, dy) for dx in MOVES for dy in ys] + [(0, dy) for dy in ys]
    barrier = pltpu.get_barrier_semaphore()
    for d in friends:
        pl.semaphore_signal(barrier, inc=1, device_id=at(d), device_id_type=MESH)

    def wait_rows(count, sem):
        whole = ready.at[pl.ds(0, count), :]
        pltpu.make_async_copy(whole, whole, sem).wait()

    sent = [0]
    due = [0, 0, 0]

    def count_rows(ref):
        total = 1
        for n in ref.shape:
            total *= n
        return total // cy

    def send(source, target, group, d):
        pltpu.make_async_remote_copy(
            src_ref=source, dst_ref=target, send_sem=send_sem.at[0], recv_sem=recv_sem.at[group],
            device_id=at(d), device_id_type=MESH,
        ).start()
        sent[0] += count_rows(source)
        due[group] += count_rows(source)

    line = iota((cx, cy), 0)
    lane = iota((cx, cy), 1)
    low_half = line < half
    middle = (lane >= cy // 4) & (lane < 3 * cy // 4)

    wait_rows(2 * tall, in_sem.at[0])
    for s in range(2):
        tiles = []
        for f in range(2):
            first, second = state[f, 0], turn(state[f, 1], half, 0)
            tiles.append(jnp.where(low_half, second, first) if s == 0 else jnp.where(low_half, first, second))
            state_pack[s, f] = tiles[f]
        diag_pack[s] = jnp.where(middle, turn(tiles[1], cy // 2, 1), tiles[0])

    pl.semaphore_wait(barrier, len(friends))

    for s, dx in enumerate(MOVES):
        send(state_pack.at[s], state_x.at[s], 1 - s, (dx, 0))
        for t, dy in enumerate(ys):
            send(diag_pack.at[s], diag_in.at[s, t], 1 - s, (dx, dy))

    wait_rows(6 * slots_all, in_sem.at[1])
    for s, (dx, side) in enumerate(zip(MOVES, (cx - 1, 0))):
        for l in range(levels):
            picked = pl.ds(l * cx + side, sd, stride=tall)
            for n in range(5):
                row_pack[s, n, pl.ds(l * sd, sd), :] = drops[n, picked, :]
            row_pack[s, 5, pl.ds(l * sd, sd), :] = perm[picked, :].astype(jnp.float32)
        send(row_pack.at[s], row_x.at[s], 2 - 2 * s, (dx, 0))
    for copy in lists:
        copy.wait()
    for s, dx in enumerate(MOVES):
        for c in range(deep):
            list_pack[s, c : c + 1, :] = lx[s : s + 1, c * cy : (c + 1) * cy].astype(jnp.float32)
        send(list_pack.at[s], list_x.at[s], 2 - 2 * s, (dx, 0))
    for s, dx in enumerate(MOVES):
        tile = None
        for n in range(6):
            for l in range(levels):
                spot = 8 * n + 4 * s + 2 * l
                moved = turn(row_pack[s, n, pl.ds(l * sd, sd), :], spot + 1, 1)
                tile = moved if tile is None else jnp.where(lane >= spot, moved, tile)
        corner_pack[s] = tile
        corner_pack[s, 0:4, note : note + kc] = lc[...].astype(jnp.float32)
        for t, dy in enumerate(ys):
            send(corner_pack.at[s], corner_in.at[s, t], 2 - 2 * s, (dx, dy))
    for t, dy in enumerate(ys):
        send(state, state_y.at[t], 0, (0, dy))
    for n in range(6):
        tile = None
        for i in range(cx):
            for l in range(levels):
                picked = pl.ds(l * cx + i, sd, stride=tall)
                value = drops[n, picked, :] if n < 5 else perm[picked, :].astype(jnp.float32)
                spot = 4 * i + 2 * l
                moved = turn(value, spot + 1, 1)
                tile = moved if tile is None else jnp.where(lane >= spot, moved, tile)
        col_pack[n] = tile
    col_pack[5, 0:2, note : note + ky] = ly[...].astype(jnp.float32)
    for t, dy in enumerate(ys):
        send(col_pack, col_in.at[t], 0, (0, dy))

    def span(n, k):
        return pl.ds(n * slots_all + k * tall, tall)

    order = [perm[k * tall : (k + 1) * tall, :] for k in range(sd)]
    for m in range(sd):
        part = pl.ds(m * tall, tall)
        weight = drops[1, part, :]
        partner = jnp.zeros((tall, cy), jnp.int32)
        first = jnp.zeros((tall, cy), jnp.int32)
        for p in range(sd):
            mine = order[p] == m
            partner = jnp.where(mine, order[p ^ 1], partner)
            if p % 2 == 0:
                first = jnp.where(mine, 1, first)
        other = drops[1, pl.ds(0, tall), :]
        for k in range(1, sd):
            other = jnp.where(partner == k, drops[1, pl.ds(k * tall, tall), :], other)
        rate, eaten = match(weight, other, first > 0)
        for n in range(3):
            bits[n, part, :] = mod(lax.shift_right_logical(partner, jnp.int32(n)), 2)
        for n, value in enumerate(prepare(drops[0, part, :], drops[2, part, :])):
            ready[span(n, m), :] = value
        east, north = drops[3, part, :], drops[4, part, :]
        ready[span(6, m), :] = jnp.abs(east - 0.5)
        ready[span(7, m), :] = jnp.abs(north - 0.5)
        ready[span(8, m), :] = rate
        ready[span(9, m), :] = eaten
        wx, wy = kernel_weights(east), kernel_weights(north)
        for a in SHIFTS:
            along = wx[a] * weight
            for b in SHIFTS:
                share[3 * a + b + 4, part, :] = wy[b] * along

    mask[...] = jnp.ones_like(mask)
    for r, side in enumerate((cx - 1, 0)):
        slots = lx[r : r + 1, :]
        hot_row = iota((rows, kx), 0) == div(slots, block)
        hot_lane = jnp.where(iota((cy, kx), 0) == mod(slots, cy), 1.0, 0.0).astype(jnp.bfloat16)
        named = lax.dot_general(
            jnp.where(hot_row, 1.0, 0.0).astype(jnp.bfloat16), hot_lane,
            (((1,), (1,)), ((), ())), preferred_element_type=jnp.float32,
        )
        mask[pl.ds(side, rows, stride=cx), :] = 1.0 - named

    width = 2 * ky + 4 * kc
    lane_e = iota((1, width), 1)
    high = (lane_e < ky) | ((lane_e >= 2 * ky) & (lane_e < 2 * ky + 2 * kc))
    high_all = jnp.broadcast_to(high, (slots_all, width))
    slots = jnp.concatenate(
        [ly[0:1, :], ly[1:2, :], lc[0:1, :], lc[2:3, :], lc[1:2, :], lc[3:4, :]], 1
    )
    hot_e = jnp.where(iota((slots_all, width), 0) == div(slots, cy), 1.0, 0.0)
    left_high = jnp.max(jnp.where(high_all, hot_e, 0.0), 1, keepdims=True)
    left_low = jnp.max(jnp.where(high_all, 0.0, hot_e), 1, keepdims=True)
    lane_all = iota((slots_all, cy), 1)
    mask[...] = mask[...] * (
        1.0 - jnp.where(lane_all == cy - 1, left_high, jnp.where(lane_all == 0, left_low, 0.0))
    )

    def land(slots, move_x, move_y):
        level = mod(div(slots, block), levels)
        i = mod(mod(div(slots, cy), cx) + move_x, cx)
        target = (level * cx + i) * cy + mod(mod(slots, cy) + move_y, cy)
        return jnp.where(slots >= 0, target, -1)

    def blend(parts, pick_second):
        return parts[0] if len(parts) == 1 else jnp.where(pick_second, parts[1], parts[0])

    left_lanes = lane < cy // 2
    keys = [(a, b) for a in SHIFTS for b in SHIFTS]

    def climate(sides):
        def beyond(l, up, down):
            return jnp.where(low_half, turn(down, half * l, 0), turn(up, half * l, 0))

        fields = []
        for f in range(2):
            fields.append([])
            for l in range(levels):
                across = beyond(l, *(state_x[s, f] for s in sides))
                far = [
                    beyond(l, *(turn(diag_in[s, t], f * (cy // 2), 1) for s in sides)) for t in range(len(ys))
                ]
                side_y = [state_y[t, f, l] for t in range(len(ys))]
                own_half = jnp.concatenate([state[f, l], across], 0)
                other_half = jnp.concatenate([blend(side_y, left_lanes), blend(far, left_lanes)], 0)
                fields[f].append(jnp.concatenate([own_half, other_half], 1))
        mixed = []
        for f in range(2):
            mixed.append([])
            for l in range(levels):
                centre = fields[f][l]
                around = turn(centre, -1, 0) + turn(centre, 1, 0) + turn(centre, -1, 1) + turn(centre, 1, 1)
                stacked = fields[f][min(l + 1, levels - 1)] + fields[f][max(l - 1, 0)]
                mixed[f].append(
                    (1.0 - 4.0 * MIX_HORIZONTAL - 2.0 * MIX_VERTICAL) * centre
                    + MIX_HORIZONTAL * around + MIX_VERTICAL * stacked
                )
        shifted = []
        terms = []
        for l in range(levels):
            vapour, warmth = mixed[0][l], mixed[1][l]
            decay = jnp.exp2((-17.27 * LOG2E) * (warmth - 273.15) / (warmth - 35.86))
            humid = (GROWTH_STEP / EXCESS_FACTOR) * (vapour * decay) - GROWTH_STEP
            shifted.append({b: turn(humid, -b, 1) for b in SHIFTS})
            terms.append(differences({(a, b): turn(shifted[l][b][:, :cy], -a, 0) for a, b in keys}))
        return mixed, shifted, terms

    def pair_up(weight, turns):
        seat = iota((sd, cy), 0)
        rank = jnp.zeros((sd, cy), jnp.int32)
        for p in range(1, sd):
            rank = jnp.where(jnp.broadcast_to(turns[p : p + 1], (sd, cy)) == seat, p, rank)
        partner = take(turns, rank ^ 1, 0)
        return partner, match(weight, take(weight, partner, 0), mod(rank, 2) == 0)

    def finish(radius, weight, dry, east, north, turns, around):
        base, top, inverse_slope, strength, lowest, cube = prepare(radius, dry)
        level = base + interpolate(around, east, north, jnp.abs(east - 0.5), jnp.abs(north - 0.5))
        root, volume = settle(level, top, inverse_slope, strength, lowest)
        partner, (rate, eaten) = pair_up(weight, turns.astype(jnp.int32))
        after, lost = collide(root, volume, take(root, partner, 0), rate, eaten)
        return weight * (volume - cube), after, weight - lost

    def side_rows(s):
        home = cx - 1 if s == 0 else 0
        fallen = []
        for l in range(levels):
            stretch = pl.ds(l * sd, sd)
            values = [row_x[s, n, stretch, :] for n in range(6)]
            around = {
                key: jnp.broadcast_to(near[l, n, home : home + 1, :], (sd, cy)) for n, key in enumerate(keys)
            }
            condensed, radius, weight = finish(*values, around)
            late_x[s, 0, stretch, :] = radius
            late_x[s, 1, stretch, :] = weight
            wx, wy = kernel_weights(values[3]), kernel_weights(values[4])
            along = wx[MOVES[s]] * condensed
            fallen.append(spread({b: jnp.sum(wy[b] * along, 0, keepdims=True) for b in SHIFTS}, 1, lane[0:1]))
        return fallen

    def side_records(s):
        slots = list_x[s].astype(jnp.int32)
        level = mod(div(slots, block), levels)
        row = jnp.where(slots >= 0, level * sd + div(slots, block * levels), -1)
        column = mod(slots, cy)
        for n in (2, 3, 4, 0, 1):
            got = jnp.zeros((deep, cy), jnp.float32)
            for r in range(rows):
                source = late_x[s, n, r : r + 1, :] if n < 2 else row_x[s, n, r : r + 1, :]
                got = jnp.where(row == r, take(jnp.broadcast_to(source, (deep, cy)), column, 1), got)
            rec_out[n, :, pl.ds(s * kx, kx)] = got.reshape(1, kx)
        box_out[:, pl.ds(s * kx, kx)] = land(slots, MOVES[s], 0).reshape(1, kx)

    wait_rows(due[0], recv_sem.at[0])
    _, _, terms = climate((1, 1))
    for l in range(levels):
        for n, key in enumerate(keys):
            near[l, n] = terms[l][key][cx:]
    arrive = [None, side_rows(1)]
    side_records(1)

    wait_rows(due[1], recv_sem.at[1])
    mixed, shifted, terms = climate((0, 1))
    window = {key: jnp.concatenate([t[key][:cx] for t in terms], 0) for key in keys}
    for l in range(levels):
        for n, key in enumerate(keys):
            near[l, n] = terms[l][key][cx:]
        moist_out[l] = mixed[0][l][:cx, :cy]
        warm_out[l] = mixed[1][l][:cx, :cy]

    odd_lane = mod(lane, 2) == 1
    second_level = mod(div(lane, 2), 2) == 1
    ends = jnp.where(odd_lane, 0, cy - 1)
    step = mod(div(lane, 4), cx)
    column = {}
    for b in SHIFTS:
        tiles = []
        for piece in (slice(0, cx), slice(cx, 2 * cx)):
            pair = [take(shifted[l][b][piece, cy:], ends, 1) for l in range(levels)]
            tiles.append(take(jnp.where(second_level, pair[1], pair[0]), step, 0))
        column[b] = jnp.where(lane < 4 * cx, tiles[0], tiles[1])
    col_terms = differences({(a, b): turn(column[b], -4 * a, 1) for a, b in keys})

    grown = []
    cubes = []
    deposit = {}
    for k in range(sd):
        part = pl.ds(k * tall, tall)
        base, top, inverse_slope, strength, lowest, cube, reach_x, reach_y = (
            ready[span(n, k), :] for n in range(8)
        )
        level = base + interpolate(window, drops[3, part, :], drops[4, part, :], reach_x, reach_y)
        root, volume = settle(level, top, inverse_slope, strength, lowest)
        gain = volume - cube
        for a, b in keys:
            term = share[3 * a + b + 4, part, :] * gain
            deposit[a, b] = term if k == 0 else deposit[a, b] + term
        grown.append(root)
        cubes.append(volume)

    own = []
    for l in range(levels):
        inner = {b: spread({a: deposit[a, b][l * cx : (l + 1) * cx] for a in SHIFTS}, 0, line) for b in SHIFTS}
        own.append(spread(inner, 1, lane))

    for m in range(sd):
        part = pl.ds(m * tall, tall)
        found = grown
        for n in range(3):
            odd = bits[n, part, :] > 0
            found = [jnp.where(odd, found[2 * i + 1], found[2 * i]) for i in range(len(found) // 2)]
        radius, lost = collide(grown[m], cubes[m], found[0], ready[span(8, m), :], ready[span(9, m), :])
        size_out[part, :] = radius
        mult_out[part, :] = mask[part, :] * (drops[1, part, :] - lost)

    wait_rows(due[2], recv_sem.at[2])
    arrive[0] = side_rows(0)

    corner = [blend([corner_in[s, t] for t in range(len(ys))], odd_lane) for s in range(2)]
    values = []
    for n in range(6):
        beside = blend([col_in[t, n] for t in range(len(ys))], odd_lane)
        below = jnp.where(lane < 4 * cx, beside, turn(corner[1], 4 * (cx - 1) - 8 * n, 1))
        values.append(jnp.where(lane >= cy - 4, turn(corner[0], cy - 4 - 8 * n, 1), below))
    condensed, radius, weight = finish(*values, col_terms)
    wx, wy = kernel_weights(values[3]), kernel_weights(values[4])
    across = jnp.where(odd_lane, wy[-1], wy[1]) * condensed
    fallen = sum(turn(jnp.sum(wx[a] * across, 0, keepdims=True), 4 * a, 1) for a in SHIFTS)
    outer = jnp.where(lane == cy - 1, 1, 0)
    for l in range(levels):
        total = own[l] + jnp.where(line == 0, arrive[0][l], jnp.where(line == cx - 1, arrive[1][l], 0.0))
        sent_in = take(jnp.broadcast_to(fallen, (cx, cy)), 4 * line + 2 * l + outer, 1)
        total = total + jnp.where((lane == 0) | (lane == cy - 1), sent_in, 0.0)
        moist_out[l] = moist_out[l] - VAPOUR_PER_SOURCE * total
        warm_out[l] = warm_out[l] + WARMING_FACTOR * total

    side_records(0)

    slots = jnp.concatenate(
        [col_in[d if len(ys) == 2 else 0, 5, d : d + 1, note : note + ky] for d in range(2)]
        + [
            corner_in[s, d if len(ys) == 2 else 0, 2 * s + d : 2 * s + d + 1, note : note + kc]
            for d in range(2) for s in range(2)
        ],
        1,
    ).astype(jnp.int32)
    face = lane_e < 2 * ky
    which = div(lane_e - 2 * ky, kc)
    minus_x = mod(which, 2)
    minus_y = jnp.where(face, jnp.where(lane_e < ky, 0, 1), div(which, 2))
    move_x = jnp.where(face, 0, 1 - 2 * minus_x)
    live = slots >= 0
    level = mod(div(slots, block), levels)
    place = jnp.where(face, mod(div(slots, cy), cx), jnp.where(minus_x == 0, cy // 4 - 1, cx))
    spot = jnp.broadcast_to(jnp.where(live, 4 * place + 2 * level + minus_y, 0), (sd, width))
    seat = iota((sd, width), 0) == jnp.where(live, div(slots, block * levels), -1)
    for n, value in enumerate((radius, weight, values[2], values[3], values[4])):
        rec_out[n, :, pl.ds(2 * kx, width)] = jnp.sum(jnp.where(seat, take(value, spot, 1), 0.0), 0, keepdims=True)
    box_out[:, pl.ds(2 * kx, width)] = land(slots, move_x, 1 - 2 * minus_y)

    wait_rows(sent[0], send_sem.at[0])


def publish(*refs):
    count = len(refs) // 2
    sems = refs[-1]
    copies = [
        pltpu.make_async_copy(refs[n], refs[count + n], sems.at[n]) for n in range(count)
    ]
    for copy in copies:
        copy.start()
    for copy in copies:
        copy.wait()


def per_device(nx, ny, moist, warm, size, mult, dry, east, north, perm, lx, ly, lc):
    levels, cx, cy = moist.shape
    sd = size.shape[0]
    kx, ky, kc = lx.shape[2], ly.shape[2], lc.shape[2]
    narr = 2 * kx + 2 * ky + 4 * kc
    slots = sd * levels * cx
    flat = [x.reshape(slots, cy) for x in (size, mult, dry, east, north, perm)]
    f32, i32 = jnp.float32, jnp.int32
    any_space = pl.BlockSpec(memory_space=pl.ANY)
    vmem_space = pl.BlockSpec(memory_space=pltpu.VMEM)
    dma = pltpu.SemaphoreType.DMA
    shapes = (
        ((levels, cx, cy), f32),
        ((levels, cx, cy), f32),
        ((slots, cy), f32),
        ((slots, cy), f32),
        ((5, 1, narr), f32),
        ((1, narr), i32),
    )
    n_y = 1 if ny == 2 else 2
    outs = pl.pallas_call(
        functools.partial(body, (levels, cx, cy, sd, kx, ky, kc, nx, ny)),
        out_shape=tuple(pltpu.VMEM(*s) for s in shapes),
        in_specs=[any_space] * 11,
        out_specs=[vmem_space] * 6,
        scratch_shapes=[
            pltpu.VMEM((2, levels, cx, cy), f32),
            pltpu.VMEM((5, slots, cy), f32),
            pltpu.VMEM((slots, cy), i32),
            pltpu.VMEM((2, kx), i32),
            pltpu.VMEM((2, ky), i32),
            pltpu.VMEM((4, kc), i32),
            pltpu.VMEM((2, 2, cx, cy), f32),
            pltpu.VMEM((2, 2, cx, cy), f32),
            pltpu.VMEM((n_y, 2, levels, cx, cy), f32),
            pltpu.VMEM((2, cx, cy), f32),
            pltpu.VMEM((2, n_y, cx, cy), f32),
            pltpu.VMEM((2, kx // cy, cy), f32),
            pltpu.VMEM((2, kx // cy, cy), f32),
            pltpu.VMEM((2, 6, sd * levels, cy), f32),
            pltpu.VMEM((2, 6, sd * levels, cy), f32),
            pltpu.VMEM((2, sd, cy), f32),
            pltpu.VMEM((2, n_y, sd, cy), f32),
            pltpu.VMEM((6, sd, cy), f32),
            pltpu.VMEM((n_y, 6, sd, cy), f32),
            pltpu.VMEM((slots, cy), f32),
            pltpu.VMEM((10 * slots, cy), f32),
            pltpu.VMEM((9, slots, cy), f32),
            pltpu.VMEM((3, slots, cy), i32),
            pltpu.VMEM((levels, 9, cx, cy), f32),
            pltpu.VMEM((2, 2, sd * levels, cy), f32),
            dma((5,)), dma((1,)), dma((3,)),
        ],
        compiler_params=pltpu.CompilerParams(collective_id=0, has_side_effects=True),
    )(moist, warm, *flat, lx, ly, lc)
    outs = pl.pallas_call(
        publish,
        out_shape=tuple(jax.ShapeDtypeStruct(*s) for s in shapes),
        in_specs=[vmem_space] * 6,
        out_specs=[any_space] * 6,
        scratch_shapes=[dma((6,))],
    )(*[pltpu.with_memory_space_constraint(x, pltpu.VMEM) for x in outs])
    return (
        outs[0], outs[1], outs[2].reshape(size.shape), outs[3].reshape(size.shape), outs[4], outs[5],
    )


def solution(mesh):
    cell, drop, lists = P(None, "gx", "gy"), P(None, None, "gx", "gy"), P("gx", None, "gy")
    return jax.shard_map(
        functools.partial(per_device, mesh.shape["gx"], mesh.shape["gy"]),
        mesh=mesh,
        in_specs=(cell,) * 2 + (drop,) * 6 + (lists,) * 3,
        out_specs=(cell, cell, drop, drop, cell, P("gx", "gy")),
        check_vma=False,
    )
```

time: 12.8 us -> 12.1 us (0.945)
  Pallas kernels: 12 us -> 11.2 us
    pallas_call x1, Pallas kernels: 11.2 us -> 10.5 us  [per_device(): pl.pallas_call(functools.partial(body, (levels, cx, cy, sd, kx, ky, kc, n...]
where the time goes in v2:
time: 12.1 us; the launch traced here: 11.9 us
  Pallas kernels  11.2 us (93%)
  between operations  0.64 us (5%)
    pallas_call x1, Pallas kernels, per_device(): pl.pallas_call(functools.partial(body, (levels, cx, cy, sd, kx, ky, kc, n...  10.5 us
    pallas_call x1, Pallas kernels, per_device(): pl.pallas_call(publish, out_shape=tuple((jax.ShapeDtypeStruct(*s) for s i...  0.73 us

profile of v2, /device:TPU:0, one launch (start us, length us, event | category | flops | bytes accessed | tf_op | source)
XLA Modules:
  0.0 11.9 jit_solution(6444283934413163635)
XLA Ops:
  0.6 10.5 %shard_map.154 = (f32[2,8,128]{2,1,0:T(8,128)S(1)}, f32[2,8,128]{2,1,0:T(8,128)S(1)}, f32[128,128]{1,0:T(8,128)S(1)}, f32[128,128]{1,0:T(8,128)S(1)}, f32[5,1,2176]{2,1,0:T(1,128)S(1)}, /*index=5*/s32[1,2176]{1,0:T(1,128)S(1)}) custom-call(f32[2,8,128]{2,1,0:T(8,128)} %moist_in.1, f32[2,8,128]{2,1,0:T(8,128)} %warm_in.1, f32[128,128]{1,0:T(8,128)} %bitcast.8, ...), custom_call_target="tpu_custom_call" | custom-call | tf_op jit(solution)/shard_map/pallas_call | solution.py:550
  11.2 0.7 %shard_map.155 = (f32[2,8,128]{2,1,0:T(8,128)}, f32[2,8,128]{2,1,0:T(8,128)}, f32[128,128]{1,0:T(8,128)}, f32[128,128]{1,0:T(8,128)}, f32[5,1,2176]{2,1,0:T(1,128)}, /*index=5*/s32[1,2176]{1,0:T(1,128)}) custom-call(f32[2,8,128]{2,1,0:T(8,128)S(1)} %get-tuple-element.18.refs_0_, f32[2,8,128]{2,1,0:T(8,128)S(1)} %get-tuple-element.19.refs_1_, ...), custom_call_target="tpu_custom_call" | custom-call | tf_op jit(solution)/shard_map/pallas_call | solution.py:585

commit v3 on v2

--- a/solution.py
+++ b/solution.py
@@ -128,11 +128,12 @@
 def body(
     sizes,
     moist_in, warm_in, size_in, mult_in, dry_in, east_in, north_in, perm_in,
+    size_cells, mult_cells, dry_cells, east_cells, north_cells, perm_cells,
     lx_in, ly_in, lc_in,
     moist_out, warm_out, size_out, mult_out, rec_out, box_out,
     state, drops, perm, lx, ly, lc,
-    state_pack, state_x, state_y, diag_pack, diag_in,
-    list_pack, list_x, row_pack, row_x, corner_pack, corner_in, col_pack, col_in,
+    state_x, state_y, diag_in, list_pack, list_x,
+    row_pack, row_x, turn_pack, turn_x, corner_pack, corner_in, col_pack, col_in,
     mask, ready, share, bits, near, late_x,
     in_sem, send_sem, recv_sem,
 ):
@@ -147,39 +148,56 @@
     tall = levels * cx
     deep = kx // cy
     note = cy // 2
+    edges = (cx - 1, 0)
+    bands = (pl.ds(cx - 3, 3), pl.ds(0, 3))
 
     def at(d):
         return (lax.rem(me_x + d[0] + nx, nx), lax.rem(me_y + d[1] + ny, ny))
-
-    for n, source in enumerate((moist_in, warm_in)):
-        pltpu.make_async_copy(source, state.at[n], in_sem.at[0]).start()
-    for n, source in enumerate((size_in, mult_in, dry_in, east_in, north_in)):
-        pltpu.make_async_copy(source, drops.at[n], in_sem.at[1]).start()
-    pltpu.make_async_copy(perm_in, perm, in_sem.at[1]).start()
-    lists = [
-        pltpu.make_async_copy(source.at[0], target, in_sem.at[2 + n])
-        for n, (source, target) in enumerate(((lx_in, lx), (ly_in, ly), (lc_in, lc)))
-    ]
-    for copy in lists:
-        copy.start()
-
-    friends = [(dx, 0) for dx in MOVES] + [(dx, dy) for dx in MOVES for dy in ys] + [(0, dy) for dy in ys]
-    barrier = pltpu.get_barrier_semaphore()
-    for d in friends:
-        pl.semaphore_signal(barrier, inc=1, device_id=at(d), device_id_type=MESH)
 
     def wait_rows(count, sem):
         whole = ready.at[pl.ds(0, count), :]
         pltpu.make_async_copy(whole, whole, sem).wait()
-
-    sent = [0]
-    due = [0, 0, 0]
 
     def count_rows(ref):
         total = 1
         for n in ref.shape:
             total *= n
         return total // cy
+
+    brought = [0, 0, 0]
+
+    def bring(source, target, group):
+        pltpu.make_async_copy(source, target, in_sem.at[group]).start()
+        brought[group] += count_rows(target)
+
+    bring(moist_in, state.at[0], 0)
+    bring(warm_in, state.at[1], 0)
+    cells = (size_cells, dry_cells, east_cells, north_cells, mult_cells)
+    for s in range(2):
+        for l in range(levels):
+            stretch = pl.ds(l * sd, sd)
+            for n, source in enumerate(cells):
+                bring(source.at[:, l, edges[s], :], row_pack.at[s, n, stretch, :], 1)
+            bring(perm_cells.at[:, l, edges[s], :], turn_pack.at[s, stretch, :], 1)
+        bring(lx_in.at[0, pl.ds(s, 1), :], list_pack.at[s], 1)
+
+    friends = [(dx, 0) for dx in MOVES] + [(dx, dy) for dx in MOVES for dy in ys] + [(0, dy) for dy in ys]
+    barrier = pltpu.get_barrier_semaphore()
+    for d in friends:
+        pl.semaphore_signal(barrier, inc=1, device_id=at(d), device_id_type=MESH)
+
+    for n, source in enumerate((size_in, mult_in, dry_in, east_in, north_in)):
+        bring(source, drops.at[n], 2)
+    bring(perm_in, perm, 2)
+    lists = [
+        pltpu.make_async_copy(source.at[0], target, in_sem.at[3 + n])
+        for n, (source, target) in enumerate(((lx_in, lx), (ly_in, ly), (lc_in, lc)))
+    ]
+    for copy in lists:
+        copy.start()
+
+    sent = [0]
+    due = [0, 0, 0, 0]
 
     def send(source, target, group, d):
         pltpu.make_async_remote_copy(
@@ -192,64 +210,63 @@
     line = iota((cx, cy), 0)
     lane = iota((cx, cy), 1)
     low_half = line < half
-    middle = (lane >= cy // 4) & (lane < 3 * cy // 4)
-
-    wait_rows(2 * tall, in_sem.at[0])
-    for s in range(2):
-        tiles = []
-        for f in range(2):
-            first, second = state[f, 0], turn(state[f, 1], half, 0)
-            tiles.append(jnp.where(low_half, second, first) if s == 0 else jnp.where(low_half, first, second))
-            state_pack[s, f] = tiles[f]
-        diag_pack[s] = jnp.where(middle, turn(tiles[1], cy // 2, 1), tiles[0])
-
-    pl.semaphore_wait(barrier, len(friends))
-
-    for s, dx in enumerate(MOVES):
-        send(state_pack.at[s], state_x.at[s], 1 - s, (dx, 0))
+
+    def send_fields(s):
+        own, far = state.at[:, :, bands[s], :], MOVES[s]
+        group = (1, 0)[s]
+        send(own, state_x.at[s, :, :, bands[s], :], group, (far, 0))
         for t, dy in enumerate(ys):
-            send(diag_pack.at[s], diag_in.at[s, t], 1 - s, (dx, dy))
-
-    wait_rows(6 * slots_all, in_sem.at[1])
-    for s, (dx, side) in enumerate(zip(MOVES, (cx - 1, 0))):
-        for l in range(levels):
-            picked = pl.ds(l * cx + side, sd, stride=tall)
-            for n in range(5):
-                row_pack[s, n, pl.ds(l * sd, sd), :] = drops[n, picked, :]
-            row_pack[s, 5, pl.ds(l * sd, sd), :] = perm[picked, :].astype(jnp.float32)
-        send(row_pack.at[s], row_x.at[s], 2 - 2 * s, (dx, 0))
-    for copy in lists:
-        copy.wait()
-    for s, dx in enumerate(MOVES):
-        for c in range(deep):
-            list_pack[s, c : c + 1, :] = lx[s : s + 1, c * cy : (c + 1) * cy].astype(jnp.float32)
-        send(list_pack.at[s], list_x.at[s], 2 - 2 * s, (dx, 0))
-    for s, dx in enumerate(MOVES):
+            send(own, diag_in.at[s, t, :, :, bands[s], :], group, (far, dy))
+
+    def send_rows(s):
+        first, second = ((2, 3), (0, 0))[s]
+        send(row_pack.at[s, 0:4], row_x.at[s, 0:4], first, (MOVES[s], 0))
+        send(list_pack.at[s], list_x.at[s], first, (MOVES[s], 0))
+        send(row_pack.at[s, 4], row_x.at[s, 4], second, (MOVES[s], 0))
+        send(turn_pack.at[s], turn_x.at[s], second, (MOVES[s], 0))
+
+    def send_corner(s):
         tile = None
         for n in range(6):
             for l in range(levels):
+                stretch = pl.ds(l * sd, sd)
+                value = row_pack[s, n, stretch, :] if n < 5 else turn_pack[s, stretch, :].astype(jnp.float32)
                 spot = 8 * n + 4 * s + 2 * l
-                moved = turn(row_pack[s, n, pl.ds(l * sd, sd), :], spot + 1, 1)
+                moved = turn(value, spot + 1, 1)
                 tile = moved if tile is None else jnp.where(lane >= spot, moved, tile)
         corner_pack[s] = tile
         corner_pack[s, 0:4, note : note + kc] = lc[...].astype(jnp.float32)
         for t, dy in enumerate(ys):
-            send(corner_pack.at[s], corner_in.at[s, t], 2 - 2 * s, (dx, dy))
+            send(corner_pack.at[s], corner_in.at[s, t], (2, 0)[s], (MOVES[s], dy))
+
+    wait_rows(brought[0], in_sem.at[0])
+    pl.semaphore_wait(barrier, len(friends))
+    send_fields(0)
+    wait_rows(brought[1], in_sem.at[1])
+    send_rows(0)
     for t, dy in enumerate(ys):
         send(state, state_y.at[t], 0, (0, dy))
+    for copy in lists:
+        copy.wait()
+    send_corner(0)
+    send_fields(1)
+    send_rows(1)
+    send_corner(1)
+    wait_rows(brought[2], in_sem.at[2])
+    attributes = (0, 2, 3, 4, 1)
     for n in range(6):
         tile = None
         for i in range(cx):
             for l in range(levels):
                 picked = pl.ds(l * cx + i, sd, stride=tall)
-                value = drops[n, picked, :] if n < 5 else perm[picked, :].astype(jnp.float32)
+                value = drops[attributes[n], picked, :] if n < 5 else perm[picked, :].astype(jnp.float32)
                 spot = 4 * i + 2 * l
                 moved = turn(value, spot + 1, 1)
                 tile = moved if tile is None else jnp.where(lane >= spot, moved, tile)
         col_pack[n] = tile
     col_pack[5, 0:2, note : note + ky] = ly[...].astype(jnp.float32)
     for t, dy in enumerate(ys):
-        send(col_pack, col_in.at[t], 0, (0, dy))
+        send(col_pack, col_in.at[t], 2, (0, dy))
 
     def span(n, k):
         return pl.ds(n * slots_all + k * tall, tall)
@@ -285,7 +302,7 @@
                 share[3 * a + b + 4, part, :] = wy[b] * along
 
     mask[...] = jnp.ones_like(mask)
-    for r, side in enumerate((cx - 1, 0)):
+    for r, side in enumerate(edges):
         slots = lx[r : r + 1, :]
         hot_row = iota((rows, kx), 0) == div(slots, block)
         hot_lane = jnp.where(iota((cy, kx), 0) == mod(slots, cy), 1.0, 0.0).astype(jnp.bfloat16)
@@ -320,24 +337,13 @@
         return parts[0] if len(parts) == 1 else jnp.where(pick_second, parts[1], parts[0])
 
     left_lanes = lane < cy // 2
+    odd_lane = mod(lane, 2) == 1
+    second_level = mod(div(lane, 2), 2) == 1
+    ends = jnp.where(odd_lane, 0, cy - 1)
+    step = mod(div(lane, 4), cx)
     keys = [(a, b) for a in SHIFTS for b in SHIFTS]
 
-    def climate(sides):
-        def beyond(l, up, down):
-            return jnp.where(low_half, turn(down, half * l, 0), turn(up, half * l, 0))
-
-        fields = []
-        for f in range(2):
-            fields.append([])
-            for l in range(levels):
-                across = beyond(l, *(state_x[s, f] for s in sides))
-                far = [
-                    beyond(l, *(turn(diag_in[s, t], f * (cy // 2), 1) for s in sides)) for t in range(len(ys))
-                ]
-                side_y = [state_y[t, f, l] for t in range(len(ys))]
-                own_half = jnp.concatenate([state[f, l], across], 0)
-                other_half = jnp.concatenate([blend(side_y, left_lanes), blend(far, left_lanes)], 0)
-                fields[f].append(jnp.concatenate([own_half, other_half], 1))
+    def climate(fields):
         mixed = []
         for f in range(2):
             mixed.append([])
@@ -359,7 +365,11 @@
             terms.append(differences({(a, b): turn(shifted[l][b][:, :cy], -a, 0) for a, b in keys}))
         return mixed, shifted, terms
 
-    def pair_up(weight, turns):
+    def columns(shifted, b, piece):
+        pair = [take(shifted[l][b][piece, cy:], ends, 1) for l in range(levels)]
+        return take(jnp.where(second_level, pair[1], pair[0]), step, 0)
+
+    def mate(weight, turns):
         seat = iota((sd, cy), 0)
         rank = jnp.zeros((sd, cy), jnp.int32)
         for p in range(1, sd):
@@ -367,73 +377,82 @@
         partner = take(turns, rank ^ 1, 0)
         return partner, match(weight, take(weight, partner, 0), mod(rank, 2) == 0)
 
-    def finish(radius, weight, dry, east, north, turns, around):
-        base, top, inverse_slope, strength, lowest, cube = prepare(radius, dry)
+    def expand(prepared, east, north, around):
+        base, top, inverse_slope, strength, lowest, cube = prepared
         level = base + interpolate(around, east, north, jnp.abs(east - 0.5), jnp.abs(north - 0.5))
         root, volume = settle(level, top, inverse_slope, strength, lowest)
-        partner, (rate, eaten) = pair_up(weight, turns.astype(jnp.int32))
+        return root, volume, volume - cube
+
+    def merge(root, volume, weight, mated):
+        partner, (rate, eaten) = mated
         after, lost = collide(root, volume, take(root, partner, 0), rate, eaten)
-        return weight * (volume - cube), after, weight - lost
-
-    def side_rows(s):
-        home = cx - 1 if s == 0 else 0
+        return after, weight - lost
+
+    def surround(l, r):
+        return {key: jnp.broadcast_to(near[l, n, r : r + 1, :], (sd, cy)) for n, key in enumerate(keys)}
+
+    def side_growth(s):
+        found = []
+        for l in range(levels):
+            radius, dry, east, north = (row_x[s, n, pl.ds(l * sd, sd), :] for n in range(4))
+            found.append(expand(prepare(radius, dry), east, north, surround(l, edges[s])))
+        return found
+
+    def side_rows(s, found):
         fallen = []
         for l in range(levels):
             stretch = pl.ds(l * sd, sd)
-            values = [row_x[s, n, stretch, :] for n in range(6)]
-            around = {
-                key: jnp.broadcast_to(near[l, n, home : home + 1, :], (sd, cy)) for n, key in enumerate(keys)
-            }
-            condensed, radius, weight = finish(*values, around)
+            root, volume, gain = found[l]
+            weight = row_x[s, 4, stretch, :]
+            radius, weight_left = merge(root, volume, weight, mate(weight, turn_x[s, stretch, :]))
             late_x[s, 0, stretch, :] = radius
-            late_x[s, 1, stretch, :] = weight
-            wx, wy = kernel_weights(values[3]), kernel_weights(values[4])
-            along = wx[MOVES[s]] * condensed
-            fallen.append(spread({b: jnp.sum(wy[b] * along, 0, keepdims=True) for b in SHIFTS}, 1, lane[0:1]))
+            late_x[s, 1, stretch, :] = weight_left
+            wx, wy = kernel_weights(row_x[s, 2, stretch, :]), kernel_weights(row_x[s, 3, stretch, :])
+            along = wx[MOVES[s]] * (weight * gain)
+            fallen.append(jnp.sum(spread({b: wy[b] * along for b in SHIFTS}, 1, lane), 0, keepdims=True))
         return fallen
 
-    def side_records(s):
-        slots = list_x[s].astype(jnp.int32)
+    def side_records(s, fields):
+        slots = list_x[s].reshape(deep, cy)
         level = mod(div(slots, block), levels)
         row = jnp.where(slots >= 0, level * sd + div(slots, block * levels), -1)
         column = mod(slots, cy)
-        for n in (2, 3, 4, 0, 1):
+        for n, source, from_n in fields:
             got = jnp.zeros((deep, cy), jnp.float32)
             for r in range(rows):
-                source = late_x[s, n, r : r + 1, :] if n < 2 else row_x[s, n, r : r + 1, :]
-                got = jnp.where(row == r, take(jnp.broadcast_to(source, (deep, cy)), column, 1), got)
+                value = jnp.broadcast_to(source[s, from_n, r : r + 1, :], (deep, cy))
+                got = jnp.where(row == r, take(value, column, 1), got)
             rec_out[n, :, pl.ds(s * kx, kx)] = got.reshape(1, kx)
-        box_out[:, pl.ds(s * kx, kx)] = land(slots, MOVES[s], 0).reshape(1, kx)
+        return slots
+
+    still = [(2, row_x, 1), (3, row_x, 2), (4, row_x, 3)]
+    moving = [(0, late_x, 0), (1, late_x, 1)]
 
     wait_rows(due[0], recv_sem.at[0])
-    _, _, terms = climate((1, 1))
-    for l in range(levels):
-        for n, key in enumerate(keys):
-            near[l, n] = terms[l][key][cx:]
-    arrive = [None, side_rows(1)]
-    side_records(1)
-
-    wait_rows(due[1], recv_sem.at[1])
-    mixed, shifted, terms = climate((0, 1))
+    fields = []
+    for f in range(2):
+        fields.append([])
+        for l in range(levels):
+            own_half = jnp.concatenate([state[f, l], state_x[1, f, l]], 0)
+            side_y = blend([state_y[t, f, l] for t in range(len(ys))], left_lanes)
+            far = blend([diag_in[1, t, f, l] for t in range(len(ys))], left_lanes)
+            fields[f].append(jnp.concatenate([own_half, jnp.concatenate([side_y, far], 0)], 1))
+    mixed, shifted, terms = climate(fields)
     window = {key: jnp.concatenate([t[key][:cx] for t in terms], 0) for key in keys}
     for l in range(levels):
         for n, key in enumerate(keys):
             near[l, n] = terms[l][key][cx:]
         moist_out[l] = mixed[0][l][:cx, :cy]
         warm_out[l] = mixed[1][l][:cx, :cy]
-
-    odd_lane = mod(lane, 2) == 1
-    second_level = mod(div(lane, 2), 2) == 1
-    ends = jnp.where(odd_lane, 0, cy - 1)
-    step = mod(div(lane, 4), cx)
-    column = {}
-    for b in SHIFTS:
-        tiles = []
-        for piece in (slice(0, cx), slice(cx, 2 * cx)):
-            pair = [take(shifted[l][b][piece, cy:], ends, 1) for l in range(levels)]
-            tiles.append(take(jnp.where(second_level, pair[1], pair[0]), step, 0))
-        column[b] = jnp.where(lane < 4 * cx, tiles[0], tiles[1])
-    col_terms = differences({(a, b): turn(column[b], -4 * a, 1) for a, b in keys})
+    inside = {
+        b: jnp.where(
+            lane < 4 * cx, columns(shifted, b, slice(0, cx)), columns(shifted, b, slice(cx, 2 * cx))
+        )
+        for b in SHIFTS
+    }
+    fallen = [None, side_rows(1, side_growth(1))]
+    slots = side_records(1, still + moving)
+    box_out[:, pl.ds(kx, kx)] = land(slots, -1, 0).reshape(1, kx)
 
     grown = []
     cubes = []
@@ -454,8 +473,11 @@
 
     own = []
     for l in range(levels):
-        inner = {b: spread({a: deposit[a, b][l * cx : (l + 1) * cx] for a in SHIFTS}, 0, line) for b in SHIFTS}
-        own.append(spread(inner, 1, lane))
+        inner = {}
+        for b in SHIFTS:
+            parts = {a: jnp.where(line < 2, 0.0, deposit[a, b][l * cx : (l + 1) * cx]) for a in SHIFTS}
+            inner[b] = spread(parts, 0, line)
+        own.append(spread(inner, 1, lane) + jnp.where(line == cx - 1, fallen[1][l], 0.0))
 
     for m in range(sd):
         part = pl.ds(m * tall, tall)
@@ -467,28 +489,76 @@
         size_out[part, :] = radius
         mult_out[part, :] = mask[part, :] * (drops[1, part, :] - lost)
 
+    redo = [(l, i) for l in range(levels) for i in range(2)]
+    waiting = {}
+    for l, i in redo:
+        picked = pl.ds(l * cx + i, sd, stride=tall)
+        radius, weight, dry, east, north = (drops[n, picked, :] for n in range(5))
+        waiting[l, i] = (
+            prepare(radius, dry), weight, east, north, mate(weight, perm[picked, :]), mask[picked, :]
+        )
+
+    wait_rows(due[1], recv_sem.at[1])
+    fields = []
+    for f in range(2):
+        fields.append([])
+        for l in range(levels):
+            side_y = blend([state_y[t, f, l] for t in range(len(ys))], left_lanes)
+            far = blend([diag_in[0, t, f, l] for t in range(len(ys))], left_lanes)
+            fields[f].append(
+                jnp.concatenate(
+                    [jnp.where(low_half, state[f, l], state_x[0, f, l]), jnp.where(low_half, side_y, far)], 1
+                )
+            )
+    mixed, shifted, terms = climate(fields)
+    fresh = (lane < 8) | (lane >= cy - 8)
+    column = {b: jnp.where(fresh, columns(shifted, b, slice(0, cx)), inside[b]) for b in SHIFTS}
+    col_terms = differences({(a, b): turn(column[b], -4 * a, 1) for a, b in keys})
+    for l in range(levels):
+        for n, key in enumerate(keys):
+            near[l, n] = terms[l][key]
+        moist_out[l, 0:1, :] = mixed[0][l][0:1, :cy]
+        warm_out[l, 0:1, :] = mixed[1][l][0:1, :cy]
+    for l in range(levels):
+        landing = [None] * 3
+        for i in range(2):
+            picked = pl.ds(l * cx + i, sd, stride=tall)
+            prepared, weight, east, north, mated, keep = waiting[l, i]
+            root, volume, gain = expand(prepared, east, north, surround(l, i))
+            radius, weight_left = merge(root, volume, weight, mated)
+            size_out[picked, :] = radius
+            mult_out[picked, :] = keep * weight_left
+            wx, wy = kernel_weights(east), kernel_weights(north)
+            for a in SHIFTS:
+                if i + a < 0:
+                    continue
+                along = wx[a] * (weight * gain)
+                parts = {b: wy[b] * along for b in SHIFTS}
+                if landing[i + a] is not None:
+                    parts = {b: parts[b] + landing[i + a][b] for b in SHIFTS}
+                landing[i + a] = parts
+        for r in range(3):
+            added = jnp.sum(spread(landing[r], 1, lane), 0, keepdims=True)
+            own[l] = own[l] + jnp.where(line == r, added, 0.0)
+
     wait_rows(due[2], recv_sem.at[2])
-    arrive[0] = side_rows(0)
-
+    side = side_growth(0)
     corner = [blend([corner_in[s, t] for t in range(len(ys))], odd_lane) for s in range(2)]
     values = []
     for n in range(6):
         beside = blend([col_in[t, n] for t in range(len(ys))], odd_lane)
         below = jnp.where(lane < 4 * cx, beside, turn(corner[1], 4 * (cx - 1) - 8 * n, 1))
         values.append(jnp.where(lane >= cy - 4, turn(corner[0], cy - 4 - 8 * n, 1), below))
-    condensed, radius, weight = finish(*values, col_terms)
-    wx, wy = kernel_weights(values[3]), kernel_weights(values[4])
-    across = jnp.where(odd_lane, wy[-1], wy[1]) * condensed
-    fallen = sum(turn(jnp.sum(wx[a] * across, 0, keepdims=True), 4 * a, 1) for a in SHIFTS)
+    radius, dry, east, north, weight, turns = values
+    root, volume, gain = expand(prepare(radius, dry), east, north, col_terms)
+    radius, weight_left = merge(root, volume, weight, mate(weight, turns.astype(jnp.int32)))
+    wx, wy = kernel_weights(east), kernel_weights(north)
+    across = jnp.where(odd_lane, wy[-1], wy[1]) * (weight * gain)
+    rain = sum(turn(jnp.sum(wx[a] * across, 0, keepdims=True), 4 * a, 1) for a in SHIFTS)
     outer = jnp.where(lane == cy - 1, 1, 0)
     for l in range(levels):
-        total = own[l] + jnp.where(line == 0, arrive[0][l], jnp.where(line == cx - 1, arrive[1][l], 0.0))
-        sent_in = take(jnp.broadcast_to(fallen, (cx, cy)), 4 * line + 2 * l + outer, 1)
-        total = total + jnp.where((lane == 0) | (lane == cy - 1), sent_in, 0.0)
-        moist_out[l] = moist_out[l] - VAPOUR_PER_SOURCE * total
-        warm_out[l] = warm_out[l] + WARMING_FACTOR * total
-
-    side_records(0)
+        sent_in = take(jnp.broadcast_to(rain, (cx, cy)), 4 * line + 2 * l + outer, 1)
+        own[l] = own[l] + jnp.where((lane == 0) | (lane == cy - 1), sent_in, 0.0)
 
     slots = jnp.concatenate(
         [col_in[d if len(ys) == 2 else 0, 5, d : d + 1, note : note + ky] for d in range(2)]
@@ -508,9 +578,19 @@
     place = jnp.where(face, mod(div(slots, cy), cx), jnp.where(minus_x == 0, cy // 4 - 1, cx))
     spot = jnp.broadcast_to(jnp.where(live, 4 * place + 2 * level + minus_y, 0), (sd, width))
     seat = iota((sd, width), 0) == jnp.where(live, div(slots, block * levels), -1)
-    for n, value in enumerate((radius, weight, values[2], values[3], values[4])):
+    for n, value in enumerate((radius, weight_left, dry, east, north)):
         rec_out[n, :, pl.ds(2 * kx, width)] = jnp.sum(jnp.where(seat, take(value, spot, 1), 0.0), 0, keepdims=True)
     box_out[:, pl.ds(2 * kx, width)] = land(slots, move_x, 1 - 2 * minus_y)
+    slots = side_records(0, still)
+    box_out[:, pl.ds(0, kx)] = land(slots, 1, 0).reshape(1, kx)
+
+    wait_rows(due[3], recv_sem.at[3])
+    fallen = side_rows(0, side)
+    for l in range(levels):
+        total = own[l] + jnp.where(line == 0, fallen[l], 0.0)
+        moist_out[l] = moist_out[l] - VAPOUR_PER_SOURCE * total
+        warm_out[l] = warm_out[l] + WARMING_FACTOR * total
+    side_records(0, moving)
 
     wait_rows(sent[0], send_sem.at[0])
 
@@ -550,7 +630,7 @@
     outs = pl.pallas_call(
         functools.partial(body, (levels, cx, cy, sd, kx, ky, kc, nx, ny)),
         out_shape=tuple(pltpu.VMEM(*s) for s in shapes),
-        in_specs=[any_space] * 11,
+        in_specs=[any_space] * 17,
         out_specs=[vmem_space] * 6,
         scratch_shapes=[
             pltpu.VMEM((2, levels, cx, cy), f32),
@@ -559,15 +639,15 @@
             pltpu.VMEM((2, kx), i32),
             pltpu.VMEM((2, ky), i32),
             pltpu.VMEM((4, kc), i32),
-            pltpu.VMEM((2, 2, cx, cy), f32),
-            pltpu.VMEM((2, 2, cx, cy), f32),
+            pltpu.VMEM((2, 2, levels, cx, cy), f32),
             pltpu.VMEM((n_y, 2, levels, cx, cy), f32),
-            pltpu.VMEM((2, cx, cy), f32),
-            pltpu.VMEM((2, n_y, cx, cy), f32),
-            pltpu.VMEM((2, kx // cy, cy), f32),
-            pltpu.VMEM((2, kx // cy, cy), f32),
-            pltpu.VMEM((2, 6, sd * levels, cy), f32),
-            pltpu.VMEM((2, 6, sd * levels, cy), f32),
+            pltpu.VMEM((2, n_y, 2, levels, cx, cy), f32),
+            pltpu.VMEM((2, 1, kx), i32),
+            pltpu.VMEM((2, 1, kx), i32),
+            pltpu.VMEM((2, 5, sd * levels, cy), f32),
+            pltpu.VMEM((2, 5, sd * levels, cy), f32),
+            pltpu.VMEM((2, sd * levels, cy), i32),
+            pltpu.VMEM((2, sd * levels, cy), i32),
             pltpu.VMEM((2, sd, cy), f32),
             pltpu.VMEM((2, n_y, sd, cy), f32),
             pltpu.VMEM((6, sd, cy), f32),
@@ -578,10 +658,10 @@
             pltpu.VMEM((3, slots, cy), i32),
             pltpu.VMEM((levels, 9, cx, cy), f32),
             pltpu.VMEM((2, 2, sd * levels, cy), f32),
-            dma((5,)), dma((1,)), dma((3,)),
+            dma((6,)), dma((1,)), dma((4,)),
         ],
         compiler_params=pltpu.CompilerParams(collective_id=0, has_side_effects=True),
-    )(moist, warm, *flat, lx, ly, lc)
+    )(moist, warm, *flat, size, mult, dry, east, north, perm, lx, ly, lc)
     outs = pl.pallas_call(
         publish,
         out_shape=tuple(jax.ShapeDtypeStruct(*s) for s in shapes),

time: 12.1 us -> 11.9 us (0.983)
    pallas_call x1, Pallas kernels: 10.5 us -> 10.4 us  [per_device(): pl.pallas_call(functools.partial(body, (levels, cx, cy, sd, kx, ky, kc, n...]
where the time goes in v3:
time: 11.9 us; the launch traced here: 11.7 us
  Pallas kernels  11.1 us (93%)
  between operations  0.64 us (5%)
    pallas_call x1, Pallas kernels, per_device(): pl.pallas_call(functools.partial(body, (levels, cx, cy, sd, kx, ky, kc, n...  10.4 us
    pallas_call x1, Pallas kernels, per_device(): pl.pallas_call(publish, out_shape=tuple((jax.ShapeDtypeStruct(*s) for s i...  0.73 us

profile of v3, /device:TPU:0, one launch (start us, length us, event | category | flops | bytes accessed | tf_op | source)
XLA Modules:
  0.0 11.7 jit_solution(1563849228741395234)
XLA Ops:
  0.6 10.4 %shard_map.154 = (f32[2,8,128]{2,1,0:T(8,128)S(1)}, f32[2,8,128]{2,1,0:T(8,128)S(1)}, f32[128,128]{1,0:T(8,128)S(1)}, f32[128,128]{1,0:T(8,128)S(1)}, f32[5,1,2176]{2,1,0:T(1,128)S(1)}, /*index=5*/s32[1,2176]{1,0:T(1,128)S(1)}) custom-call(f32[2,8,128]{2,1,0:T(8,128)} %moist_in.1, f32[2,8,128]{2,1,0:T(8,128)} %warm_in.1, f32[128,128]{1,0:T(8,128)} %bitcast.8, ...), custom_call_target="tpu_custom_call" | custom-call | tf_op jit(solution)/shard_map/pallas_call | solution.py:630
  11.0 0.7 %shard_map.155 = (f32[2,8,128]{2,1,0:T(8,128)}, f32[2,8,128]{2,1,0:T(8,128)}, f32[128,128]{1,0:T(8,128)}, f32[128,128]{1,0:T(8,128)}, f32[5,1,2176]{2,1,0:T(1,128)}, /*index=5*/s32[1,2176]{1,0:T(1,128)}) custom-call(f32[2,8,128]{2,1,0:T(8,128)S(1)} %get-tuple-element.18.refs_0_, f32[2,8,128]{2,1,0:T(8,128)S(1)} %get-tuple-element.19.refs_1_, ...), custom_call_target="tpu_custom_call" | custom-call | tf_op jit(solution)/shard_map/pallas_call | solution.py:665

commit v4 on v3

--- a/solution.py
+++ b/solution.py
@@ -65,22 +65,25 @@
     return (
         area - (GROWTH_STEP * CURVATURE) * inverse,
         (5.0 / 3.0) * pull,
-        1.0 / (1.0 + pull * square),
+        1.0 + pull * square,
         strength,
         lowest,
         area * radius,
     )
 
 
-def settle(level, top, inverse_slope, strength, lowest):
-    wetted = jnp.maximum((level + top) * inverse_slope, lowest)
+def settle(level, top, bottom, strength, lowest):
+    above = jnp.maximum(level + top, lowest * bottom)
+    flat = lax.rsqrt(above * bottom)
     for sweep in range(NEWTON - 1):
-        inverse_root = lax.rsqrt(wetted)
+        inverse_root = bottom * flat
         square = inverse_root * inverse_root
         pull = strength * (square * inverse_root)
-        wetted = jnp.maximum((level + (5.0 / 3.0) * pull) / (1.0 + pull * square), lowest)
-    root = wetted * lax.rsqrt(wetted)
-    return root, wetted * root
+        bottom = 1.0 + pull * square
+        above = jnp.maximum(level + (5.0 / 3.0) * pull, lowest * bottom)
+        flat = lax.rsqrt(above * bottom)
+    root = above * flat
+    return root, (root * root) * root
 
 
 def differences(near):
@@ -131,10 +134,10 @@
     size_cells, mult_cells, dry_cells, east_cells, north_cells, perm_cells,
     lx_in, ly_in, lc_in,
     moist_out, warm_out, size_out, mult_out, rec_out, box_out,
-    state, drops, perm, lx, ly, lc,
+    state, drops, perm, ly, lc,
     state_x, state_y, diag_in, list_pack, list_x,
     row_pack, row_x, turn_pack, turn_x, corner_pack, corner_in, col_pack, col_in,
-    mask, ready, share, bits, near, late_x,
+    mask, ready, share, bits, near, near_up, late_x, fall,
     in_sem, send_sem, recv_sem,
 ):
     levels, cx, cy, sd, kx, ky, kc, nx, ny = sizes
@@ -147,7 +150,6 @@
     block = cx * cy
     tall = levels * cx
     deep = kx // cy
-    note = cy // 2
     edges = (cx - 1, 0)
     bands = (pl.ds(cx - 3, 3), pl.ds(0, 3))
 
@@ -164,7 +166,7 @@
             total *= n
         return total // cy
 
-    brought = [0, 0, 0]
+    brought = [0, 0, 0, 0]
 
     def bring(source, target, group):
         pltpu.make_async_copy(source, target, in_sem.at[group]).start()
@@ -173,31 +175,39 @@
     bring(moist_in, state.at[0], 0)
     bring(warm_in, state.at[1], 0)
     cells = (size_cells, dry_cells, east_cells, north_cells, mult_cells)
-    for s in range(2):
-        for l in range(levels):
-            stretch = pl.ds(l * sd, sd)
-            for n, source in enumerate(cells):
-                bring(source.at[:, l, edges[s], :], row_pack.at[s, n, stretch, :], 1)
-            bring(perm_cells.at[:, l, edges[s], :], turn_pack.at[s, stretch, :], 1)
-        bring(lx_in.at[0, pl.ds(s, 1), :], list_pack.at[s], 1)
+
+    def bring_rows(s, chosen, group):
+        for n in chosen:
+            for l in range(levels):
+                stretch = pl.ds(l * sd, sd)
+                if n < 5:
+                    bring(cells[n].at[:, l, edges[s], :], row_pack.at[s, n, stretch, :], group)
+                else:
+                    bring(perm_cells.at[:, l, edges[s], :], turn_pack.at[s, stretch, :], group)
+
+    bring_rows(0, range(4), 1)
 
     friends = [(dx, 0) for dx in MOVES] + [(dx, dy) for dx in MOVES for dy in ys] + [(0, dy) for dy in ys]
     barrier = pltpu.get_barrier_semaphore()
     for d in friends:
         pl.semaphore_signal(barrier, inc=1, device_id=at(d), device_id_type=MESH)
 
-    for n, source in enumerate((size_in, mult_in, dry_in, east_in, north_in)):
-        bring(source, drops.at[n], 2)
-    bring(perm_in, perm, 2)
+    bring_rows(0, (4, 5), 2)
+    for s in range(2):
+        bring(lx_in.at[0, pl.ds(s, 1), :], list_pack.at[s], 2)
+    bring_rows(1, range(6), 2)
     lists = [
-        pltpu.make_async_copy(source.at[0], target, in_sem.at[3 + n])
-        for n, (source, target) in enumerate(((lx_in, lx), (ly_in, ly), (lc_in, lc)))
+        pltpu.make_async_copy(source.at[0], target, in_sem.at[4 + n])
+        for n, (source, target) in enumerate(((ly_in, ly), (lc_in, lc)))
     ]
     for copy in lists:
         copy.start()
+    for n, source in enumerate((size_in, mult_in, dry_in, east_in, north_in)):
+        bring(source, drops.at[n], 3)
+    bring(perm_in, perm, 3)
 
     sent = [0]
-    due = [0, 0, 0, 0]
+    due = [0] * 6
 
     def send(source, target, group, d):
         pltpu.make_async_remote_copy(
@@ -218,12 +228,13 @@
         for t, dy in enumerate(ys):
             send(own, diag_in.at[s, t, :, :, bands[s], :], group, (far, dy))
 
-    def send_rows(s):
-        first, second = ((2, 3), (0, 0))[s]
-        send(row_pack.at[s, 0:4], row_x.at[s, 0:4], first, (MOVES[s], 0))
-        send(list_pack.at[s], list_x.at[s], first, (MOVES[s], 0))
-        send(row_pack.at[s, 4], row_x.at[s, 4], second, (MOVES[s], 0))
-        send(turn_pack.at[s], turn_x.at[s], second, (MOVES[s], 0))
+    def send_growth(s):
+        send(row_pack.at[s, 0:4], row_x.at[s, 0:4], (4, 3)[s], (MOVES[s], 0))
+
+    def send_rest(s):
+        send(row_pack.at[s, 4], row_x.at[s, 4], (5, 3)[s], (MOVES[s], 0))
+        send(turn_pack.at[s], turn_x.at[s], (5, 3)[s], (MOVES[s], 0))
+        send(list_pack.at[s], list_x.at[s], (5, 3)[s], (MOVES[s], 0))
 
     def send_corner(s):
         tile = None
@@ -235,24 +246,31 @@
                 moved = turn(value, spot + 1, 1)
                 tile = moved if tile is None else jnp.where(lane >= spot, moved, tile)
         corner_pack[s] = tile
-        corner_pack[s, 0:4, note : note + kc] = lc[...].astype(jnp.float32)
+        for d in range(2):
+            spot = 2 * ky + kc * (2 * d + s)
+            corner_pack[s, 2 * s + d : 2 * s + d + 1, spot : spot + kc] = lc[
+                2 * s + d : 2 * s + d + 1, :
+            ].astype(jnp.float32)
         for t, dy in enumerate(ys):
-            send(corner_pack.at[s], corner_in.at[s, t], (2, 0)[s], (MOVES[s], dy))
+            send(corner_pack.at[s], corner_in.at[s, t], 2, (MOVES[s], dy))
 
     wait_rows(brought[0], in_sem.at[0])
     pl.semaphore_wait(barrier, len(friends))
     send_fields(0)
     wait_rows(brought[1], in_sem.at[1])
-    send_rows(0)
+    send_growth(0)
     for t, dy in enumerate(ys):
         send(state, state_y.at[t], 0, (0, dy))
+    wait_rows(brought[2], in_sem.at[2])
+    send_rest(0)
     for copy in lists:
         copy.wait()
+    send_fields(1)
     send_corner(0)
-    send_fields(1)
-    send_rows(1)
+    send_growth(1)
+    send_rest(1)
     send_corner(1)
-    wait_rows(brought[2], in_sem.at[2])
+    wait_rows(brought[3], in_sem.at[3])
     attributes = (0, 2, 3, 4, 1)
     for n in range(6):
         tile = None
@@ -264,7 +282,8 @@
                 moved = turn(value, spot + 1, 1)
                 tile = moved if tile is None else jnp.where(lane >= spot, moved, tile)
         col_pack[n] = tile
-    col_pack[5, 0:2, note : note + ky] = ly[...].astype(jnp.float32)
+    for d in range(2):
+        col_pack[6, d : d + 1, d * ky : (d + 1) * ky] = ly[d : d + 1, :].astype(jnp.float32)
     for t, dy in enumerate(ys):
         send(col_pack, col_in.at[t], 2, (0, dy))
 
@@ -303,7 +322,7 @@
 
     mask[...] = jnp.ones_like(mask)
     for r, side in enumerate(edges):
-        slots = lx[r : r + 1, :]
+        slots = list_pack[r]
         hot_row = iota((rows, kx), 0) == div(slots, block)
         hot_lane = jnp.where(iota((cy, kx), 0) == mod(slots, cy), 1.0, 0.0).astype(jnp.bfloat16)
         named = lax.dot_general(
@@ -338,36 +357,63 @@
 
     left_lanes = lane < cy // 2
     odd_lane = mod(lane, 2) == 1
-    second_level = mod(div(lane, 2), 2) == 1
-    ends = jnp.where(odd_lane, 0, cy - 1)
-    step = mod(div(lane, 4), cx)
+    group = div(lane, 4)
     keys = [(a, b) for a in SHIFTS for b in SHIFTS]
 
     def climate(fields):
-        mixed = []
-        for f in range(2):
-            mixed.append([])
+        deep_lane = iota(fields[0][0][0].shape, 1)
+        odd = mod(deep_lane, 2) == 1
+
+        def fixed(value, spot):
+            return take(value, jnp.full(value.shape, spot, jnp.int32), 1)
+
+        def reach(own, other, s):
+            if s == 0:
+                return own
+            inside = deep_lane < cy - s if s > 0 else deep_lane >= -s
+            return jnp.where(inside, turn(own, -s, 1), turn(other, -s, 1))
+
+        def brink(own, other, s):
+            if s == 0:
+                return take(other, jnp.where(odd, 0, cy - 1), 1)
+            if s > 0:
+                return jnp.where(odd, fixed(other, s), fixed(own, s - 1))
+            return jnp.where(odd, fixed(own, cy + s), fixed(other, cy - 1 + s))
+
+        def humidity(cut):
+            raw = [[{s: cut(*fields[f][l], s) for s in range(-2, 3)} for l in range(levels)] for f in range(2)]
+            mixed = []
+            for f in range(2):
+                mixed.append([])
+                for l in range(levels):
+                    at_shift = {}
+                    for b in SHIFTS:
+                        centre = raw[f][l][b]
+                        around = raw[f][l][b - 1] + raw[f][l][b + 1] + (turn(centre, -1, 0) + turn(centre, 1, 0))
+                        stacked = raw[f][min(l + 1, levels - 1)][b] + raw[f][max(l - 1, 0)][b]
+                        at_shift[b] = (
+                            (1.0 - 4.0 * MIX_HORIZONTAL - 2.0 * MIX_VERTICAL) * centre
+                            + MIX_HORIZONTAL * around + MIX_VERTICAL * stacked
+                        )
+                    mixed[f].append(at_shift)
+            humid = []
             for l in range(levels):
-                centre = fields[f][l]
-                around = turn(centre, -1, 0) + turn(centre, 1, 0) + turn(centre, -1, 1) + turn(centre, 1, 1)
-                stacked = fields[f][min(l + 1, levels - 1)] + fields[f][max(l - 1, 0)]
-                mixed[f].append(
-                    (1.0 - 4.0 * MIX_HORIZONTAL - 2.0 * MIX_VERTICAL) * centre
-                    + MIX_HORIZONTAL * around + MIX_VERTICAL * stacked
-                )
-        shifted = []
-        terms = []
-        for l in range(levels):
-            vapour, warmth = mixed[0][l], mixed[1][l]
-            decay = jnp.exp2((-17.27 * LOG2E) * (warmth - 273.15) / (warmth - 35.86))
-            humid = (GROWTH_STEP / EXCESS_FACTOR) * (vapour * decay) - GROWTH_STEP
-            shifted.append({b: turn(humid, -b, 1) for b in SHIFTS})
-            terms.append(differences({(a, b): turn(shifted[l][b][:, :cy], -a, 0) for a, b in keys}))
-        return mixed, shifted, terms
-
-    def columns(shifted, b, piece):
-        pair = [take(shifted[l][b][piece, cy:], ends, 1) for l in range(levels)]
-        return take(jnp.where(second_level, pair[1], pair[0]), step, 0)
+                humid.append({})
+                for b in SHIFTS:
+                    warmth = mixed[1][l][b]
+                    decay = jnp.exp2((-17.27 * LOG2E) * (warmth - 273.15) / (warmth - 35.86))
+                    humid[l][b] = (GROWTH_STEP / EXCESS_FACTOR) * (mixed[0][l][b] * decay) - GROWTH_STEP
+            return mixed, humid
+
+        mixed, humid = humidity(reach)
+        terms = [differences({(a, b): turn(humid[l][b], -a, 0) for a, b in keys}) for l in range(levels)]
+        _, column = humidity(brink)
+        wide_level = mod(div(deep_lane, 2), 2) == 1
+        column = {b: jnp.where(wide_level, column[1][b], column[0][b]) for b in SHIFTS}
+        return mixed, terms, column
+
+    def from_row(value, a):
+        return take(value, mod(group + a, cx), 0)
 
     def mate(weight, turns):
         seat = iota((sd, cy), 0)
@@ -378,9 +424,9 @@
         return partner, match(weight, take(weight, partner, 0), mod(rank, 2) == 0)
 
     def expand(prepared, east, north, around):
-        base, top, inverse_slope, strength, lowest, cube = prepared
+        base, top, bottom, strength, lowest, cube = prepared
         level = base + interpolate(around, east, north, jnp.abs(east - 0.5), jnp.abs(north - 0.5))
-        root, volume = settle(level, top, inverse_slope, strength, lowest)
+        root, volume = settle(level, top, bottom, strength, lowest)
         return root, volume, volume - cube
 
     def merge(root, volume, weight, mated):
@@ -388,18 +434,19 @@
         after, lost = collide(root, volume, take(root, partner, 0), rate, eaten)
         return after, weight - lost
 
-    def surround(l, r):
-        return {key: jnp.broadcast_to(near[l, n, r : r + 1, :], (sd, cy)) for n, key in enumerate(keys)}
+    def surround(ref, l, r):
+        return {key: jnp.broadcast_to(ref[l, n, r : r + 1, :], (sd, cy)) for n, key in enumerate(keys)}
 
     def side_growth(s):
+        ref, r = ((near, cx - 1), (near_up, 0))[s]
         found = []
         for l in range(levels):
             radius, dry, east, north = (row_x[s, n, pl.ds(l * sd, sd), :] for n in range(4))
-            found.append(expand(prepare(radius, dry), east, north, surround(l, edges[s])))
+            found.append(expand(prepare(radius, dry), east, north, surround(ref, l, r)))
         return found
 
     def side_rows(s, found):
-        fallen = []
+        home = (0, cx - 1)[s]
         for l in range(levels):
             stretch = pl.ds(l * sd, sd)
             root, volume, gain = found[l]
@@ -409,61 +456,55 @@
             late_x[s, 1, stretch, :] = weight_left
             wx, wy = kernel_weights(row_x[s, 2, stretch, :]), kernel_weights(row_x[s, 3, stretch, :])
             along = wx[MOVES[s]] * (weight * gain)
-            fallen.append(jnp.sum(spread({b: wy[b] * along for b in SHIFTS}, 1, lane), 0, keepdims=True))
-        return fallen
-
-    def side_records(s, fields):
+            for b in SHIFTS:
+                fall[b + 1, l, home : home + 1, :] += jnp.sum(wy[b] * along, 0, keepdims=True)
+
+    def side_records(s):
         slots = list_x[s].reshape(deep, cy)
         level = mod(div(slots, block), levels)
         row = jnp.where(slots >= 0, level * sd + div(slots, block * levels), -1)
         column = mod(slots, cy)
+        fields = [(2, row_x, 1), (3, row_x, 2), (4, row_x, 3), (0, late_x, 0), (1, late_x, 1)]
         for n, source, from_n in fields:
             got = jnp.zeros((deep, cy), jnp.float32)
             for r in range(rows):
                 value = jnp.broadcast_to(source[s, from_n, r : r + 1, :], (deep, cy))
                 got = jnp.where(row == r, take(value, column, 1), got)
             rec_out[n, :, pl.ds(s * kx, kx)] = got.reshape(1, kx)
-        return slots
-
-    still = [(2, row_x, 1), (3, row_x, 2), (4, row_x, 3)]
-    moving = [(0, late_x, 0), (1, late_x, 1)]
+        box_out[:, pl.ds(s * kx, kx)] = land(slots, MOVES[s], 0).reshape(1, kx)
 
     wait_rows(due[0], recv_sem.at[0])
     fields = []
     for f in range(2):
         fields.append([])
         for l in range(levels):
-            own_half = jnp.concatenate([state[f, l], state_x[1, f, l]], 0)
             side_y = blend([state_y[t, f, l] for t in range(len(ys))], left_lanes)
             far = blend([diag_in[1, t, f, l] for t in range(len(ys))], left_lanes)
-            fields[f].append(jnp.concatenate([own_half, jnp.concatenate([side_y, far], 0)], 1))
-    mixed, shifted, terms = climate(fields)
+            fields[f].append(
+                (jnp.concatenate([state[f, l], state_x[1, f, l]], 0), jnp.concatenate([side_y, far], 0))
+            )
+    mixed, terms, column = climate(fields)
     window = {key: jnp.concatenate([t[key][:cx] for t in terms], 0) for key in keys}
     for l in range(levels):
         for n, key in enumerate(keys):
-            near[l, n] = terms[l][key][cx:]
-        moist_out[l] = mixed[0][l][:cx, :cy]
-        warm_out[l] = mixed[1][l][:cx, :cy]
+            near_up[l, n] = terms[l][key][cx:]
+        moist_out[l] = mixed[0][l][0][:cx]
+        warm_out[l] = mixed[1][l][0][:cx]
     inside = {
-        b: jnp.where(
-            lane < 4 * cx, columns(shifted, b, slice(0, cx)), columns(shifted, b, slice(cx, 2 * cx))
+        (a, b): jnp.where(
+            mod(group + a, cy // 4) < cx, from_row(column[b][:cx], a), from_row(column[b][cx:], a)
         )
-        for b in SHIFTS
+        for a, b in keys
     }
-    fallen = [None, side_rows(1, side_growth(1))]
-    slots = side_records(1, still + moving)
-    box_out[:, pl.ds(kx, kx)] = land(slots, -1, 0).reshape(1, kx)
 
     grown = []
     cubes = []
     deposit = {}
     for k in range(sd):
         part = pl.ds(k * tall, tall)
-        base, top, inverse_slope, strength, lowest, cube, reach_x, reach_y = (
-            ready[span(n, k), :] for n in range(8)
-        )
+        base, top, bottom, strength, lowest, cube, reach_x, reach_y = (ready[span(n, k), :] for n in range(8))
         level = base + interpolate(window, drops[3, part, :], drops[4, part, :], reach_x, reach_y)
-        root, volume = settle(level, top, inverse_slope, strength, lowest)
+        root, volume = settle(level, top, bottom, strength, lowest)
         gain = volume - cube
         for a, b in keys:
             term = share[3 * a + b + 4, part, :] * gain
@@ -471,13 +512,10 @@
         grown.append(root)
         cubes.append(volume)
 
-    own = []
     for l in range(levels):
-        inner = {}
         for b in SHIFTS:
             parts = {a: jnp.where(line < 2, 0.0, deposit[a, b][l * cx : (l + 1) * cx]) for a in SHIFTS}
-            inner[b] = spread(parts, 0, line)
-        own.append(spread(inner, 1, lane) + jnp.where(line == cx - 1, fallen[1][l], 0.0))
+            fall[b + 1, l] = spread(parts, 0, line)
 
     for m in range(sd):
         part = pl.ds(m * tall, tall)
@@ -489,6 +527,13 @@
         size_out[part, :] = radius
         mult_out[part, :] = mask[part, :] * (drops[1, part, :] - lost)
 
+    def upper_side():
+        wait_rows(due[3], recv_sem.at[3])
+        side_rows(1, side_growth(1))
+        side_records(1)
+
+    pl.when(me_x != nx - 1)(upper_side)
+
     redo = [(l, i) for l in range(levels) for i in range(2)]
     waiting = {}
     for l, i in redo:
@@ -506,25 +551,26 @@
             side_y = blend([state_y[t, f, l] for t in range(len(ys))], left_lanes)
             far = blend([diag_in[0, t, f, l] for t in range(len(ys))], left_lanes)
             fields[f].append(
-                jnp.concatenate(
-                    [jnp.where(low_half, state[f, l], state_x[0, f, l]), jnp.where(low_half, side_y, far)], 1
-                )
+                (jnp.where(low_half, state[f, l], state_x[0, f, l]), jnp.where(low_half, side_y, far))
             )
-    mixed, shifted, terms = climate(fields)
-    fresh = (lane < 8) | (lane >= cy - 8)
-    column = {b: jnp.where(fresh, columns(shifted, b, slice(0, cx)), inside[b]) for b in SHIFTS}
-    col_terms = differences({(a, b): turn(column[b], -4 * a, 1) for a, b in keys})
+    mixed, terms, column = climate(fields)
     for l in range(levels):
         for n, key in enumerate(keys):
             near[l, n] = terms[l][key]
-        moist_out[l, 0:1, :] = mixed[0][l][0:1, :cy]
-        warm_out[l, 0:1, :] = mixed[1][l][0:1, :cy]
+        moist_out[l, 0:1, :] = mixed[0][l][0][0:1]
+        warm_out[l, 0:1, :] = mixed[1][l][0][0:1]
+    col_terms = differences(
+        {
+            (a, b): jnp.where(mod(group + a + 2, cy // 4) < 4, from_row(column[b], a), inside[a, b])
+            for a, b in keys
+        }
+    )
     for l in range(levels):
         landing = [None] * 3
         for i in range(2):
             picked = pl.ds(l * cx + i, sd, stride=tall)
             prepared, weight, east, north, mated, keep = waiting[l, i]
-            root, volume, gain = expand(prepared, east, north, surround(l, i))
+            root, volume, gain = expand(prepared, east, north, surround(near, l, i))
             radius, weight_left = merge(root, volume, weight, mated)
             size_out[picked, :] = radius
             mult_out[picked, :] = keep * weight_left
@@ -538,11 +584,10 @@
                     parts = {b: parts[b] + landing[i + a][b] for b in SHIFTS}
                 landing[i + a] = parts
         for r in range(3):
-            added = jnp.sum(spread(landing[r], 1, lane), 0, keepdims=True)
-            own[l] = own[l] + jnp.where(line == r, added, 0.0)
+            for b in SHIFTS:
+                fall[b + 1, l, r : r + 1, :] += jnp.sum(landing[r][b], 0, keepdims=True)
 
     wait_rows(due[2], recv_sem.at[2])
-    side = side_growth(0)
     corner = [blend([corner_in[s, t] for t in range(len(ys))], odd_lane) for s in range(2)]
     values = []
     for n in range(6):
@@ -554,24 +599,25 @@
     radius, weight_left = merge(root, volume, weight, mate(weight, turns.astype(jnp.int32)))
     wx, wy = kernel_weights(east), kernel_weights(north)
     across = jnp.where(odd_lane, wy[-1], wy[1]) * (weight * gain)
-    rain = sum(turn(jnp.sum(wx[a] * across, 0, keepdims=True), 4 * a, 1) for a in SHIFTS)
+    rain = {a: jnp.broadcast_to(jnp.sum(wx[a] * across, 0, keepdims=True), (cx, cy)) for a in SHIFTS}
     outer = jnp.where(lane == cy - 1, 1, 0)
+    edge_fall = []
     for l in range(levels):
-        sent_in = take(jnp.broadcast_to(rain, (cx, cy)), 4 * line + 2 * l + outer, 1)
-        own[l] = own[l] + jnp.where((lane == 0) | (lane == cy - 1), sent_in, 0.0)
-
-    slots = jnp.concatenate(
-        [col_in[d if len(ys) == 2 else 0, 5, d : d + 1, note : note + ky] for d in range(2)]
-        + [
-            corner_in[s, d if len(ys) == 2 else 0, 2 * s + d : 2 * s + d + 1, note : note + kc]
-            for d in range(2) for s in range(2)
-        ],
-        1,
-    ).astype(jnp.int32)
-    face = lane_e < 2 * ky
+        sent_in = sum(take(rain[a], mod(4 * (line - a) + 2 * l + outer, cy), 1) for a in SHIFTS)
+        edge_fall.append(jnp.where((lane == 0) | (lane == cy - 1), sent_in, 0.0))
+
     which = div(lane_e - 2 * ky, kc)
     minus_x = mod(which, 2)
+    face = lane_e < 2 * ky
     minus_y = jnp.where(face, jnp.where(lane_e < ky, 0, 1), div(which, 2))
+    slots = None
+    for d in range(2):
+        t = d if len(ys) == 2 else 0
+        faces = col_in[t, 6, d : d + 1, :]
+        corners = [corner_in[s, t, 2 * s + d : 2 * s + d + 1, :] for s in range(2)]
+        found = jnp.where(face, faces, jnp.where(minus_x == 0, corners[0], corners[1]))
+        slots = found if d == 0 else jnp.where(minus_y == 0, slots, found)
+    slots = slots.astype(jnp.int32)
     move_x = jnp.where(face, 0, 1 - 2 * minus_x)
     live = slots >= 0
     level = mod(div(slots, block), levels)
@@ -581,16 +627,19 @@
     for n, value in enumerate((radius, weight_left, dry, east, north)):
         rec_out[n, :, pl.ds(2 * kx, width)] = jnp.sum(jnp.where(seat, take(value, spot, 1), 0.0), 0, keepdims=True)
     box_out[:, pl.ds(2 * kx, width)] = land(slots, move_x, 1 - 2 * minus_y)
-    slots = side_records(0, still)
-    box_out[:, pl.ds(0, kx)] = land(slots, 1, 0).reshape(1, kx)
-
-    wait_rows(due[3], recv_sem.at[3])
-    fallen = side_rows(0, side)
+
+    wait_rows(due[4], recv_sem.at[4])
+    side = side_growth(0)
+    wait_rows(due[5], recv_sem.at[5])
+    side_rows(0, side)
+    side_records(0)
+
+    pl.when(me_x == nx - 1)(upper_side)
+
     for l in range(levels):
-        total = own[l] + jnp.where(line == 0, fallen[l], 0.0)
+        total = spread({b: fall[b + 1, l] for b in SHIFTS}, 1, lane) + edge_fall[l]
         moist_out[l] = moist_out[l] - VAPOUR_PER_SOURCE * total
         warm_out[l] = warm_out[l] + WARMING_FACTOR * total
-    side_records(0, moving)
 
     wait_rows(sent[0], send_sem.at[0])
 
@@ -636,7 +685,6 @@
             pltpu.VMEM((2, levels, cx, cy), f32),
             pltpu.VMEM((5, slots, cy), f32),
             pltpu.VMEM((slots, cy), i32),
-            pltpu.VMEM((2, kx), i32),
             pltpu.VMEM((2, ky), i32),
             pltpu.VMEM((4, kc), i32),
             pltpu.VMEM((2, 2, levels, cx, cy), f32),
@@ -650,15 +698,17 @@
             pltpu.VMEM((2, sd * levels, cy), i32),
             pltpu.VMEM((2, sd, cy), f32),
             pltpu.VMEM((2, n_y, sd, cy), f32),
-            pltpu.VMEM((6, sd, cy), f32),
-            pltpu.VMEM((n_y, 6, sd, cy), f32),
+            pltpu.VMEM((7, sd, cy), f32),
+            pltpu.VMEM((n_y, 7, sd, cy), f32),
             pltpu.VMEM((slots, cy), f32),
             pltpu.VMEM((10 * slots, cy), f32),
             pltpu.VMEM((9, slots, cy), f32),
             pltpu.VMEM((3, slots, cy), i32),
             pltpu.VMEM((levels, 9, cx, cy), f32),
+            pltpu.VMEM((levels, 9, cx, cy), f32),
             pltpu.VMEM((2, 2, sd * levels, cy), f32),
-            dma((6,)), dma((1,)), dma((4,)),
+            pltpu.VMEM((3, levels, cx, cy), f32),
+            dma((6,)), dma((1,)), dma((6,)),
         ],
         compiler_params=pltpu.CompilerParams(collective_id=0, has_side_effects=True),
     )(moist, warm, *flat, size, mult, dry, east, north, perm, lx, ly, lc)

time: 11.9 us -> 11.9 us (level)
  no operation moved by 1% of the time
where the time goes in v4:
time: 11.9 us; the launch traced here: 11.7 us
  Pallas kernels  11 us (92%)
  between operations  0.64 us (5%)
    pallas_call x1, Pallas kernels, per_device(): pl.pallas_call(functools.partial(body, (levels, cx, cy, sd, kx, ky, kc, n...  10.3 us
    pallas_call x1, Pallas kernels, per_device(): pl.pallas_call(publish, out_shape=tuple((jax.ShapeDtypeStruct(*s) for s i...  0.73 us

profile of v4, /device:TPU:0, one launch (start us, length us, event | category | flops | bytes accessed | tf_op | source)
XLA Modules:
  0.0 11.7 jit_solution(1087062245792267081)
XLA Ops:
  0.6 10.3 %shard_map.154 = (f32[2,8,128]{2,1,0:T(8,128)S(1)}, f32[2,8,128]{2,1,0:T(8,128)S(1)}, f32[128,128]{1,0:T(8,128)S(1)}, f32[128,128]{1,0:T(8,128)S(1)}, f32[5,1,2176]{2,1,0:T(1,128)S(1)}, /*index=5*/s32[1,2176]{1,0:T(1,128)S(1)}) custom-call(f32[2,8,128]{2,1,0:T(8,128)} %moist_in.1, f32[2,8,128]{2,1,0:T(8,128)} %warm_in.1, f32[128,128]{1,0:T(8,128)} %bitcast.8, ...), custom_call_target="tpu_custom_call" | custom-call | tf_op jit(solution)/shard_map/pallas_call | solution.py:679
  11.0 0.7 %shard_map.155 = (f32[2,8,128]{2,1,0:T(8,128)}, f32[2,8,128]{2,1,0:T(8,128)}, f32[128,128]{1,0:T(8,128)}, f32[128,128]{1,0:T(8,128)}, f32[5,1,2176]{2,1,0:T(1,128)}, /*index=5*/s32[1,2176]{1,0:T(1,128)}) custom-call(f32[2,8,128]{2,1,0:T(8,128)S(1)} %get-tuple-element.18.refs_0_, f32[2,8,128]{2,1,0:T(8,128)S(1)} %get-tuple-element.19.refs_1_, ...), custom_call_target="tpu_custom_call" | custom-call | tf_op jit(solution)/shard_map/pallas_call | solution.py:715

commit v5 on v4

--- a/solution.py
+++ b/solution.py
@@ -135,10 +135,10 @@
     lx_in, ly_in, lc_in,
     moist_out, warm_out, size_out, mult_out, rec_out, box_out,
     state, drops, perm, ly, lc,
-    state_x, state_y, diag_in, list_pack, list_x,
-    row_pack, row_x, turn_pack, turn_x, corner_pack, corner_in, col_pack, col_in,
+    state_x, state_y, diag_in, list_pack, list_sort, list_x,
+    row_pack, row_sort, row_x, turn_pack, rank_of, corner_pack, corner_in, col_pack, col_in,
     mask, ready, share, bits, near, near_up, late_x, fall,
-    in_sem, send_sem, recv_sem,
+    in_sem, send_sem, recv_sem, lower_in,
 ):
     levels, cx, cy, sd, kx, ky, kc, nx, ny = sizes
     me_x = lax.axis_index("gx")
@@ -172,8 +172,6 @@
         pltpu.make_async_copy(source, target, in_sem.at[group]).start()
         brought[group] += count_rows(target)
 
-    bring(moist_in, state.at[0], 0)
-    bring(warm_in, state.at[1], 0)
     cells = (size_cells, dry_cells, east_cells, north_cells, mult_cells)
 
     def bring_rows(s, chosen, group):
@@ -185,17 +183,18 @@
                 else:
                     bring(perm_cells.at[:, l, edges[s], :], turn_pack.at[s, stretch, :], group)
 
-    bring_rows(0, range(4), 1)
-
-    friends = [(dx, 0) for dx in MOVES] + [(dx, dy) for dx in MOVES for dy in ys] + [(0, dy) for dy in ys]
+    bring_rows(0, (5, 0, 1, 2, 3, 4), 1)
+    bring(lx_in.at[0, pl.ds(0, 1), :], list_pack.at[0], 1)
+    bring(moist_in, state.at[0], 0)
+    bring(warm_in, state.at[1], 0)
+
+    beside = [0] + list(ys)
     barrier = pltpu.get_barrier_semaphore()
-    for d in friends:
+    for d in [(-1, dy) for dy in beside] + [(0, dy) for dy in ys]:
         pl.semaphore_signal(barrier, inc=1, device_id=at(d), device_id_type=MESH)
 
-    bring_rows(0, (4, 5), 2)
-    for s in range(2):
-        bring(lx_in.at[0, pl.ds(s, 1), :], list_pack.at[s], 2)
     bring_rows(1, range(6), 2)
+    bring(lx_in.at[0, pl.ds(1, 1), :], list_pack.at[1], 2)
     lists = [
         pltpu.make_async_copy(source.at[0], target, in_sem.at[4 + n])
         for n, (source, target) in enumerate(((ly_in, ly), (lc_in, lc)))
@@ -207,7 +206,7 @@
     bring(perm_in, perm, 3)
 
     sent = [0]
-    due = [0] * 6
+    due = [0] * 7
 
     def send(source, target, group, d):
         pltpu.make_async_remote_copy(
@@ -228,13 +227,32 @@
         for t, dy in enumerate(ys):
             send(own, diag_in.at[s, t, :, :, bands[s], :], group, (far, dy))
 
-    def send_growth(s):
-        send(row_pack.at[s, 0:4], row_x.at[s, 0:4], (4, 3)[s], (MOVES[s], 0))
-
-    def send_rest(s):
-        send(row_pack.at[s, 4], row_x.at[s, 4], (5, 3)[s], (MOVES[s], 0))
-        send(turn_pack.at[s], turn_x.at[s], (5, 3)[s], (MOVES[s], 0))
-        send(list_pack.at[s], list_x.at[s], (5, 3)[s], (MOVES[s], 0))
+    seat = iota((sd, cy), 0)
+
+    def send_rows(s):
+        for l in range(levels):
+            stretch = pl.ds(l * sd, sd)
+            turns = turn_pack[s, stretch, :]
+            for n in range(5):
+                row_sort[s, n, stretch, :] = take(row_pack[s, n, stretch, :], turns, 0)
+        send(row_sort.at[s, 0:4], row_x.at[s, 0:4], (4, 3)[s], (MOVES[s], 0))
+        send(row_sort.at[s, 4], row_x.at[s, 4], (5, 3)[s], (MOVES[s], 0))
+        for l in range(levels):
+            rank = jnp.zeros((sd, cy), jnp.int32)
+            for p in range(1, sd):
+                here = jnp.broadcast_to(turn_pack[s, l * sd + p : l * sd + p + 1, :], (sd, cy)) == seat
+                rank = jnp.where(here, p, rank)
+            rank_of[s, pl.ds(l * sd, sd), :] = rank
+        slots = list_pack[s].reshape(deep, cy)
+        k = div(slots, block * levels)
+        row = mod(div(slots, block), levels) * sd + k
+        place = jnp.zeros((deep, cy), jnp.int32)
+        for r in range(rows):
+            value = take(jnp.broadcast_to(rank_of[s, r : r + 1, :], (deep, cy)), mod(slots, cy), 1)
+            place = jnp.where(row == r, value, place)
+        moved = jnp.where(slots >= 0, slots + (place - k) * (block * levels), -1)
+        list_sort[s] = moved.reshape(1, kx)
+        send(list_sort.at[s], list_x.at[s], (6, 3)[s], (MOVES[s], 0))
 
     def send_corner(s):
         tile = None
@@ -254,22 +272,22 @@
         for t, dy in enumerate(ys):
             send(corner_pack.at[s], corner_in.at[s, t], 2, (MOVES[s], dy))
 
+    pl.semaphore_wait(barrier, len(beside) + len(ys))
+    for dy in beside:
+        for f, source in enumerate((moist_in, warm_in)):
+            target = state_x.at[0] if dy == 0 else diag_in.at[0, ys.index(dy)]
+            send(source.at[:, bands[0], :], target.at[f, :, bands[0], :], 1, (1, dy))
+    for dy in beside:
+        pl.semaphore_signal(lower_in, inc=1, device_id=at((1, dy)), device_id_type=MESH)
+    wait_rows(brought[1], in_sem.at[1])
+    send_rows(0)
+    for copy in lists:
+        copy.wait()
+    send_corner(0)
     wait_rows(brought[0], in_sem.at[0])
-    pl.semaphore_wait(barrier, len(friends))
-    send_fields(0)
-    wait_rows(brought[1], in_sem.at[1])
-    send_growth(0)
     for t, dy in enumerate(ys):
         send(state, state_y.at[t], 0, (0, dy))
     wait_rows(brought[2], in_sem.at[2])
-    send_rest(0)
-    for copy in lists:
-        copy.wait()
-    send_fields(1)
-    send_corner(0)
-    send_growth(1)
-    send_rest(1)
-    send_corner(1)
     wait_rows(brought[3], in_sem.at[3])
     attributes = (0, 2, 3, 4, 1)
     for n in range(6):
@@ -416,7 +434,6 @@
         return take(value, mod(group + a, cx), 0)
 
     def mate(weight, turns):
-        seat = iota((sd, cy), 0)
         rank = jnp.zeros((sd, cy), jnp.int32)
         for p in range(1, sd):
             rank = jnp.where(jnp.broadcast_to(turns[p : p + 1], (sd, cy)) == seat, p, rank)
@@ -428,6 +445,11 @@
         level = base + interpolate(around, east, north, jnp.abs(east - 0.5), jnp.abs(north - 0.5))
         root, volume = settle(level, top, bottom, strength, lowest)
         return root, volume, volume - cube
+
+    across_pair = seat ^ 1
+
+    def pair(weight):
+        return across_pair, match(weight, take(weight, across_pair, 0), mod(seat, 2) == 0)
 
     def merge(root, volume, weight, mated):
         partner, (rate, eaten) = mated
@@ -451,7 +473,7 @@
             stretch = pl.ds(l * sd, sd)
             root, volume, gain = found[l]
             weight = row_x[s, 4, stretch, :]
-            radius, weight_left = merge(root, volume, weight, mate(weight, turn_x[s, stretch, :]))
+            radius, weight_left = merge(root, volume, weight, pair(weight))
             late_x[s, 0, stretch, :] = radius
             late_x[s, 1, stretch, :] = weight_left
             wx, wy = kernel_weights(row_x[s, 2, stretch, :]), kernel_weights(row_x[s, 3, stretch, :])
@@ -472,6 +494,11 @@
                 got = jnp.where(row == r, take(value, column, 1), got)
             rec_out[n, :, pl.ds(s * kx, kx)] = got.reshape(1, kx)
         box_out[:, pl.ds(s * kx, kx)] = land(slots, MOVES[s], 0).reshape(1, kx)
+
+    pl.semaphore_wait(lower_in, len(beside))
+    send_fields(1)
+    send_rows(1)
+    send_corner(1)
 
     wait_rows(due[0], recv_sem.at[0])
     fields = []
@@ -623,19 +650,18 @@
     level = mod(div(slots, block), levels)
     place = jnp.where(face, mod(div(slots, cy), cx), jnp.where(minus_x == 0, cy // 4 - 1, cx))
     spot = jnp.broadcast_to(jnp.where(live, 4 * place + 2 * level + minus_y, 0), (sd, width))
-    seat = iota((sd, width), 0) == jnp.where(live, div(slots, block * levels), -1)
+    chosen = iota((sd, width), 0) == jnp.where(live, div(slots, block * levels), -1)
     for n, value in enumerate((radius, weight_left, dry, east, north)):
-        rec_out[n, :, pl.ds(2 * kx, width)] = jnp.sum(jnp.where(seat, take(value, spot, 1), 0.0), 0, keepdims=True)
+        rec_out[n, :, pl.ds(2 * kx, width)] = jnp.sum(jnp.where(chosen, take(value, spot, 1), 0.0), 0, keepdims=True)
     box_out[:, pl.ds(2 * kx, width)] = land(slots, move_x, 1 - 2 * minus_y)
 
     wait_rows(due[4], recv_sem.at[4])
     side = side_growth(0)
+    pl.when(me_x == nx - 1)(upper_side)
     wait_rows(due[5], recv_sem.at[5])
     side_rows(0, side)
+    wait_rows(due[6], recv_sem.at[6])
     side_records(0)
-
-    pl.when(me_x == nx - 1)(upper_side)
-
     for l in range(levels):
         total = spread({b: fall[b + 1, l] for b in SHIFTS}, 1, lane) + edge_fall[l]
         moist_out[l] = moist_out[l] - VAPOUR_PER_SOURCE * total
@@ -692,6 +718,8 @@
             pltpu.VMEM((2, n_y, 2, levels, cx, cy), f32),
             pltpu.VMEM((2, 1, kx), i32),
             pltpu.VMEM((2, 1, kx), i32),
+            pltpu.VMEM((2, 1, kx), i32),
+            pltpu.VMEM((2, 5, sd * levels, cy), f32),
             pltpu.VMEM((2, 5, sd * levels, cy), f32),
             pltpu.VMEM((2, 5, sd * levels, cy), f32),
             pltpu.VMEM((2, sd * levels, cy), i32),
@@ -708,7 +736,7 @@
             pltpu.VMEM((levels, 9, cx, cy), f32),
             pltpu.VMEM((2, 2, sd * levels, cy), f32),
             pltpu.VMEM((3, levels, cx, cy), f32),
-            dma((6,)), dma((1,)), dma((6,)),
+            dma((6,)), dma((1,)), dma((7,)), pltpu.SemaphoreType.REGULAR,
         ],
         compiler_params=pltpu.CompilerParams(collective_id=0, has_side_effects=True),
     )(moist, warm, *flat, size, mult, dry, east, north, perm, lx, ly, lc)

time: 11.9 us -> 11.7 us (0.983)
    pallas_call x1, Pallas kernels: 10.3 us -> 10.2 us  [per_device(): pl.pallas_call(functools.partial(body, (levels, cx, cy, sd, kx, ky, kc, n...]
where the time goes in v5:
time: 11.7 us; the launch traced here: 11.5 us
  Pallas kernels  10.9 us (93%)
  between operations  0.64 us (5%)
    pallas_call x1, Pallas kernels, per_device(): pl.pallas_call(functools.partial(body, (levels, cx, cy, sd, kx, ky, kc, n...  10.2 us
    pallas_call x1, Pallas kernels, per_device(): pl.pallas_call(publish, out_shape=tuple((jax.ShapeDtypeStruct(*s) for s i...  0.73 us

profile of v5, /device:TPU:0, one launch (start us, length us, event | category | flops | bytes accessed | tf_op | source)
XLA Modules:
  0.0 11.5 jit_solution(11691352683230924199)
XLA Ops:
  0.6 10.2 %shard_map.154 = (f32[2,8,128]{2,1,0:T(8,128)S(1)}, f32[2,8,128]{2,1,0:T(8,128)S(1)}, f32[128,128]{1,0:T(8,128)S(1)}, f32[128,128]{1,0:T(8,128)S(1)}, f32[5,1,2176]{2,1,0:T(1,128)S(1)}, /*index=5*/s32[1,2176]{1,0:T(1,128)S(1)}) custom-call(f32[2,8,128]{2,1,0:T(8,128)} %moist_in.1, f32[2,8,128]{2,1,0:T(8,128)} %warm_in.1, f32[128,128]{1,0:T(8,128)} %bitcast.8, ...), custom_call_target="tpu_custom_call" | custom-call | tf_op jit(solution)/shard_map/pallas_call | solution.py:705
  10.8 0.7 %shard_map.155 = (f32[2,8,128]{2,1,0:T(8,128)}, f32[2,8,128]{2,1,0:T(8,128)}, f32[128,128]{1,0:T(8,128)}, f32[128,128]{1,0:T(8,128)}, f32[5,1,2176]{2,1,0:T(1,128)}, /*index=5*/s32[1,2176]{1,0:T(1,128)}) custom-call(f32[2,8,128]{2,1,0:T(8,128)S(1)} %get-tuple-element.18.refs_0_, f32[2,8,128]{2,1,0:T(8,128)S(1)} %get-tuple-element.19.refs_1_, ...), custom_call_target="tpu_custom_call" | custom-call | tf_op jit(solution)/shard_map/pallas_call | solution.py:743

commit v6 on v5

--- a/solution.py
+++ b/solution.py
@@ -137,7 +137,7 @@
     state, drops, perm, ly, lc,
     state_x, state_y, diag_in, list_pack, list_sort, list_x,
     row_pack, row_sort, row_x, turn_pack, rank_of, corner_pack, corner_in, col_pack, col_in,
-    mask, ready, share, bits, near, near_up, late_x, fall,
+    mask, ready, share, bits, near, near_up, late_x, fall, brink_fall,
     in_sem, send_sem, recv_sem, lower_in,
 ):
     levels, cx, cy, sd, kx, ky, kc, nx, ny = sizes
@@ -166,7 +166,7 @@
             total *= n
         return total // cy
 
-    brought = [0, 0, 0, 0]
+    brought = [0, 0, 0]
 
     def bring(source, target, group):
         pltpu.make_async_copy(source, target, in_sem.at[group]).start()
@@ -183,8 +183,9 @@
                 else:
                     bring(perm_cells.at[:, l, edges[s], :], turn_pack.at[s, stretch, :], group)
 
-    bring_rows(0, (5, 0, 1, 2, 3, 4), 1)
-    bring(lx_in.at[0, pl.ds(0, 1), :], list_pack.at[0], 1)
+    bring_rows(0, (5, 0, 1), 1)
+    bring_rows(0, (2, 3, 4), 2)
+    bring(lx_in.at[0, pl.ds(0, 1), :], list_pack.at[0], 2)
     bring(moist_in, state.at[0], 0)
     bring(warm_in, state.at[1], 0)
 
@@ -193,17 +194,17 @@
     for d in [(-1, dy) for dy in beside] + [(0, dy) for dy in ys]:
         pl.semaphore_signal(barrier, inc=1, device_id=at(d), device_id_type=MESH)
 
-    bring_rows(1, range(6), 2)
-    bring(lx_in.at[0, pl.ds(1, 1), :], list_pack.at[1], 2)
+    bring_rows(1, range(6), 0)
+    bring(lx_in.at[0, pl.ds(1, 1), :], list_pack.at[1], 0)
     lists = [
-        pltpu.make_async_copy(source.at[0], target, in_sem.at[4 + n])
+        pltpu.make_async_copy(source.at[0], target, in_sem.at[3 + n])
         for n, (source, target) in enumerate(((ly_in, ly), (lc_in, lc)))
     ]
     for copy in lists:
         copy.start()
     for n, source in enumerate((size_in, mult_in, dry_in, east_in, north_in)):
-        bring(source, drops.at[n], 3)
-    bring(perm_in, perm, 3)
+        bring(source, drops.at[n], 0)
+    bring(perm_in, perm, 0)
 
     sent = [0]
     due = [0] * 7
@@ -229,13 +230,20 @@
 
     seat = iota((sd, cy), 0)
 
-    def send_rows(s):
+    def sort_rows(s, chosen):
         for l in range(levels):
             stretch = pl.ds(l * sd, sd)
             turns = turn_pack[s, stretch, :]
-            for n in range(5):
+            for n in chosen:
                 row_sort[s, n, stretch, :] = take(row_pack[s, n, stretch, :], turns, 0)
-        send(row_sort.at[s, 0:4], row_x.at[s, 0:4], (4, 3)[s], (MOVES[s], 0))
+
+    def send_first(s):
+        sort_rows(s, (0, 1))
+        send(row_sort.at[s, 0:2], row_x.at[s, 0:2], (4, 3)[s], (MOVES[s], 0))
+
+    def send_rows(s):
+        sort_rows(s, (2, 3, 4))
+        send(row_sort.at[s, 2:4], row_x.at[s, 2:4], (4, 3)[s], (MOVES[s], 0))
         send(row_sort.at[s, 4], row_x.at[s, 4], (5, 3)[s], (MOVES[s], 0))
         for l in range(levels):
             rank = jnp.zeros((sd, cy), jnp.int32)
@@ -280,6 +288,8 @@
     for dy in beside:
         pl.semaphore_signal(lower_in, inc=1, device_id=at((1, dy)), device_id_type=MESH)
     wait_rows(brought[1], in_sem.at[1])
+    send_first(0)
+    wait_rows(brought[2], in_sem.at[2])
     send_rows(0)
     for copy in lists:
         copy.wait()
@@ -287,8 +297,6 @@
     wait_rows(brought[0], in_sem.at[0])
     for t, dy in enumerate(ys):
         send(state, state_y.at[t], 0, (0, dy))
-    wait_rows(brought[2], in_sem.at[2])
-    wait_rows(brought[3], in_sem.at[3])
     attributes = (0, 2, 3, 4, 1)
     for n in range(6):
         tile = None
@@ -497,6 +505,7 @@
 
     pl.semaphore_wait(lower_in, len(beside))
     send_fields(1)
+    send_first(1)
     send_rows(1)
     send_corner(1)
 
@@ -614,72 +623,84 @@
             for b in SHIFTS:
                 fall[b + 1, l, r : r + 1, :] += jnp.sum(landing[r][b], 0, keepdims=True)
 
-    wait_rows(due[2], recv_sem.at[2])
-    corner = [blend([corner_in[s, t] for t in range(len(ys))], odd_lane) for s in range(2)]
-    values = []
-    for n in range(6):
-        beside = blend([col_in[t, n] for t in range(len(ys))], odd_lane)
-        below = jnp.where(lane < 4 * cx, beside, turn(corner[1], 4 * (cx - 1) - 8 * n, 1))
-        values.append(jnp.where(lane >= cy - 4, turn(corner[0], cy - 4 - 8 * n, 1), below))
-    radius, dry, east, north, weight, turns = values
-    root, volume, gain = expand(prepare(radius, dry), east, north, col_terms)
-    radius, weight_left = merge(root, volume, weight, mate(weight, turns.astype(jnp.int32)))
-    wx, wy = kernel_weights(east), kernel_weights(north)
-    across = jnp.where(odd_lane, wy[-1], wy[1]) * (weight * gain)
-    rain = {a: jnp.broadcast_to(jnp.sum(wx[a] * across, 0, keepdims=True), (cx, cy)) for a in SHIFTS}
-    outer = jnp.where(lane == cy - 1, 1, 0)
-    edge_fall = []
-    for l in range(levels):
-        sent_in = sum(take(rain[a], mod(4 * (line - a) + 2 * l + outer, cy), 1) for a in SHIFTS)
-        edge_fall.append(jnp.where((lane == 0) | (lane == cy - 1), sent_in, 0.0))
-
-    which = div(lane_e - 2 * ky, kc)
-    minus_x = mod(which, 2)
-    face = lane_e < 2 * ky
-    minus_y = jnp.where(face, jnp.where(lane_e < ky, 0, 1), div(which, 2))
-    slots = None
-    for d in range(2):
-        t = d if len(ys) == 2 else 0
-        faces = col_in[t, 6, d : d + 1, :]
-        corners = [corner_in[s, t, 2 * s + d : 2 * s + d + 1, :] for s in range(2)]
-        found = jnp.where(face, faces, jnp.where(minus_x == 0, corners[0], corners[1]))
-        slots = found if d == 0 else jnp.where(minus_y == 0, slots, found)
-    slots = slots.astype(jnp.int32)
-    move_x = jnp.where(face, 0, 1 - 2 * minus_x)
-    live = slots >= 0
-    level = mod(div(slots, block), levels)
-    place = jnp.where(face, mod(div(slots, cy), cx), jnp.where(minus_x == 0, cy // 4 - 1, cx))
-    spot = jnp.broadcast_to(jnp.where(live, 4 * place + 2 * level + minus_y, 0), (sd, width))
-    chosen = iota((sd, width), 0) == jnp.where(live, div(slots, block * levels), -1)
-    for n, value in enumerate((radius, weight_left, dry, east, north)):
-        rec_out[n, :, pl.ds(2 * kx, width)] = jnp.sum(jnp.where(chosen, take(value, spot, 1), 0.0), 0, keepdims=True)
-    box_out[:, pl.ds(2 * kx, width)] = land(slots, move_x, 1 - 2 * minus_y)
-
-    wait_rows(due[4], recv_sem.at[4])
-    side = side_growth(0)
     pl.when(me_x == nx - 1)(upper_side)
-    wait_rows(due[5], recv_sem.at[5])
-    side_rows(0, side)
-    wait_rows(due[6], recv_sem.at[6])
-    side_records(0)
-    for l in range(levels):
-        total = spread({b: fall[b + 1, l] for b in SHIFTS}, 1, lane) + edge_fall[l]
-        moist_out[l] = moist_out[l] - VAPOUR_PER_SOURCE * total
-        warm_out[l] = warm_out[l] + WARMING_FACTOR * total
+
+    def columns():
+        wait_rows(due[2], recv_sem.at[2])
+        corner = [blend([corner_in[s, t] for t in range(len(ys))], odd_lane) for s in range(2)]
+        values = []
+        for n in range(6):
+            beside = blend([col_in[t, n] for t in range(len(ys))], odd_lane)
+            below = jnp.where(lane < 4 * cx, beside, turn(corner[1], 4 * (cx - 1) - 8 * n, 1))
+            values.append(jnp.where(lane >= cy - 4, turn(corner[0], cy - 4 - 8 * n, 1), below))
+        radius, dry, east, north, weight, turns = values
+        root, volume, gain = expand(prepare(radius, dry), east, north, col_terms)
+        radius, weight_left = merge(root, volume, weight, mate(weight, turns.astype(jnp.int32)))
+        wx, wy = kernel_weights(east), kernel_weights(north)
+        across = jnp.where(odd_lane, wy[-1], wy[1]) * (weight * gain)
+        rain = {a: jnp.broadcast_to(jnp.sum(wx[a] * across, 0, keepdims=True), (cx, cy)) for a in SHIFTS}
+        outer = jnp.where(lane == cy - 1, 1, 0)
+        for l in range(levels):
+            sent_in = sum(take(rain[a], mod(4 * (line - a) + 2 * l + outer, cy), 1) for a in SHIFTS)
+            brink_fall[l] = jnp.where((lane == 0) | (lane == cy - 1), sent_in, 0.0)
+
+        which = div(lane_e - 2 * ky, kc)
+        minus_x = mod(which, 2)
+        face = lane_e < 2 * ky
+        minus_y = jnp.where(face, jnp.where(lane_e < ky, 0, 1), div(which, 2))
+        slots = None
+        for d in range(2):
+            t = d if len(ys) == 2 else 0
+            faces = col_in[t, 6, d : d + 1, :]
+            corners = [corner_in[s, t, 2 * s + d : 2 * s + d + 1, :] for s in range(2)]
+            found = jnp.where(face, faces, jnp.where(minus_x == 0, corners[0], corners[1]))
+            slots = found if d == 0 else jnp.where(minus_y == 0, slots, found)
+        slots = slots.astype(jnp.int32)
+        move_x = jnp.where(face, 0, 1 - 2 * minus_x)
+        live = slots >= 0
+        level = mod(div(slots, block), levels)
+        place = jnp.where(face, mod(div(slots, cy), cx), jnp.where(minus_x == 0, cy // 4 - 1, cx))
+        spot = jnp.broadcast_to(jnp.where(live, 4 * place + 2 * level + minus_y, 0), (sd, width))
+        chosen = iota((sd, width), 0) == jnp.where(live, div(slots, block * levels), -1)
+        for n, value in enumerate((radius, weight_left, dry, east, north)):
+            rec_out[n, :, pl.ds(2 * kx, width)] = jnp.sum(jnp.where(chosen, take(value, spot, 1), 0.0), 0, keepdims=True)
+        box_out[:, pl.ds(2 * kx, width)] = land(slots, move_x, 1 - 2 * minus_y)
+
+    def rows_below():
+        wait_rows(due[4], recv_sem.at[4])
+        side = side_growth(0)
+        wait_rows(due[5], recv_sem.at[5])
+        side_rows(0, side)
+        wait_rows(due[6], recv_sem.at[6])
+        side_records(0)
+
+    def total_up():
+        for l in range(levels):
+            total = spread({b: fall[b + 1, l] for b in SHIFTS}, 1, lane) + brink_fall[l]
+            moist_out[l] = moist_out[l] - VAPOUR_PER_SOURCE * total
+            warm_out[l] = warm_out[l] + WARMING_FACTOR * total
+
+    @pl.when(me_y == 0)
+    def _():
+        columns()
+        rows_below()
+        total_up()
+
+    @pl.when(me_y != 0)
+    def _():
+        rows_below()
+        columns()
+        total_up()
 
     wait_rows(sent[0], send_sem.at[0])
 
 
 def publish(*refs):
-    count = len(refs) // 2
-    sems = refs[-1]
-    copies = [
-        pltpu.make_async_copy(refs[n], refs[count + n], sems.at[n]) for n in range(count)
-    ]
-    for copy in copies:
-        copy.start()
-    for copy in copies:
-        copy.wait()
+    whole, sem = refs[-2:]
+    count = len(refs) // 2 - 1
+    for n in range(count):
+        pltpu.make_async_copy(refs[n], refs[count + n], sem).start()
+    pltpu.make_async_copy(whole, whole, sem).wait()
 
 
 def per_device(nx, ny, moist, warm, size, mult, dry, east, north, perm, lx, ly, lc):
@@ -702,6 +723,7 @@
         ((1, narr), i32),
     )
     n_y = 1 if ny == 2 else 2
+    total = 2 * levels * cx + 2 * slots + 6 * narr // cy
     outs = pl.pallas_call(
         functools.partial(body, (levels, cx, cy, sd, kx, ky, kc, nx, ny)),
         out_shape=tuple(pltpu.VMEM(*s) for s in shapes),
@@ -736,7 +758,8 @@
             pltpu.VMEM((levels, 9, cx, cy), f32),
             pltpu.VMEM((2, 2, sd * levels, cy), f32),
             pltpu.VMEM((3, levels, cx, cy), f32),
-            dma((6,)), dma((1,)), dma((7,)), pltpu.SemaphoreType.REGULAR,
+            pltpu.VMEM((levels, cx, cy), f32),
+            dma((5,)), dma((1,)), dma((7,)), pltpu.SemaphoreType.REGULAR,
         ],
         compiler_params=pltpu.CompilerParams(collective_id=0, has_side_effects=True),
     )(moist, warm, *flat, size, mult, dry, east, north, perm, lx, ly, lc)
@@ -745,7 +768,7 @@
         out_shape=tuple(jax.ShapeDtypeStruct(*s) for s in shapes),
         in_specs=[vmem_space] * 6,
         out_specs=[any_space] * 6,
-        scratch_shapes=[dma((6,))],
+        scratch_shapes=[pltpu.VMEM((total, cy), f32), dma],
     )(*[pltpu.with_memory_space_constraint(x, pltpu.VMEM) for x in outs])
     return (
         outs[0], outs[1], outs[2].reshape(size.shape), outs[3].reshape(size.shape), outs[4], outs[5],

time: 11.7 us -> 11.6 us (level)
  no operation moved by 1% of the time
where the time goes in v6:
time: 11.6 us; the launch traced here: 11.5 us
  Pallas kernels  10.8 us (93%)
  between operations  0.64 us (6%)
    pallas_call x1, Pallas kernels, per_device(): pl.pallas_call(functools.partial(body, (levels, cx, cy, sd, kx, ky, kc, n...  10.1 us
    pallas_call x1, Pallas kernels, per_device(): pl.pallas_call(publish, out_shape=tuple((jax.ShapeDtypeStruct(*s) for s i...  0.68 us

profile of v6, /device:TPU:0, one launch (start us, length us, event | category | flops | bytes accessed | tf_op | source)
XLA Modules:
  0.0 11.5 jit_solution(11300132967149062184)
XLA Ops:
  0.6 10.1 %shard_map.154 = (f32[2,8,128]{2,1,0:T(8,128)S(1)}, f32[2,8,128]{2,1,0:T(8,128)S(1)}, f32[128,128]{1,0:T(8,128)S(1)}, f32[128,128]{1,0:T(8,128)S(1)}, f32[5,1,2176]{2,1,0:T(1,128)S(1)}, /*index=5*/s32[1,2176]{1,0:T(1,128)S(1)}) custom-call(f32[2,8,128]{2,1,0:T(8,128)} %moist_in.1, f32[2,8,128]{2,1,0:T(8,128)} %warm_in.1, f32[128,128]{1,0:T(8,128)} %bitcast.8, ...), custom_call_target="tpu_custom_call" | custom-call | tf_op jit(solution)/shard_map/pallas_call | solution.py:727
  10.8 0.7 %shard_map.155 = (f32[2,8,128]{2,1,0:T(8,128)}, f32[2,8,128]{2,1,0:T(8,128)}, f32[128,128]{1,0:T(8,128)}, f32[128,128]{1,0:T(8,128)}, f32[5,1,2176]{2,1,0:T(1,128)}, /*index=5*/s32[1,2176]{1,0:T(1,128)}) custom-call(f32[2,8,128]{2,1,0:T(8,128)S(1)} %get-tuple-element.18.refs_0_, f32[2,8,128]{2,1,0:T(8,128)S(1)} %get-tuple-element.19.refs_1_, ...), custom_call_target="tpu_custom_call" | custom-call | tf_op jit(solution)/shard_map/pallas_call | solution.py:766

commit v7 on v6

--- a/solution.py
+++ b/solution.py
@@ -230,6 +230,20 @@
 
     seat = iota((sd, cy), 0)
 
+    def look_up(load_row, row, column):
+        groups = 2
+        found = [None] * groups
+        for m in range(rows // groups):
+            for n in range(groups):
+                r = n * (rows // groups) + m
+                value = take(jnp.broadcast_to(load_row(r), (deep, cy)), column, 1)
+                found[n] = value if m == 0 else jnp.where(row == r, value, found[n])
+        while len(found) > 1:
+            size = rows // len(found)
+            odd = mod(div(row, size), 2) == 1
+            found = [jnp.where(odd, found[2 * m + 1], found[2 * m]) for m in range(len(found) // 2)]
+        return found[0]
+
     def sort_rows(s, chosen):
         for l in range(levels):
             stretch = pl.ds(l * sd, sd)
@@ -254,10 +268,7 @@
         slots = list_pack[s].reshape(deep, cy)
         k = div(slots, block * levels)
         row = mod(div(slots, block), levels) * sd + k
-        place = jnp.zeros((deep, cy), jnp.int32)
-        for r in range(rows):
-            value = take(jnp.broadcast_to(rank_of[s, r : r + 1, :], (deep, cy)), mod(slots, cy), 1)
-            place = jnp.where(row == r, value, place)
+        place = look_up(lambda r: rank_of[s, r : r + 1, :], row, mod(slots, cy))
         moved = jnp.where(slots >= 0, slots + (place - k) * (block * levels), -1)
         list_sort[s] = moved.reshape(1, kx)
         send(list_sort.at[s], list_x.at[s], (6, 3)[s], (MOVES[s], 0))
@@ -492,15 +503,13 @@
     def side_records(s):
         slots = list_x[s].reshape(deep, cy)
         level = mod(div(slots, block), levels)
-        row = jnp.where(slots >= 0, level * sd + div(slots, block * levels), -1)
+        live = slots >= 0
+        row = level * sd + div(slots, block * levels)
         column = mod(slots, cy)
         fields = [(2, row_x, 1), (3, row_x, 2), (4, row_x, 3), (0, late_x, 0), (1, late_x, 1)]
         for n, source, from_n in fields:
-            got = jnp.zeros((deep, cy), jnp.float32)
-            for r in range(rows):
-                value = jnp.broadcast_to(source[s, from_n, r : r + 1, :], (deep, cy))
-                got = jnp.where(row == r, take(value, column, 1), got)
-            rec_out[n, :, pl.ds(s * kx, kx)] = got.reshape(1, kx)
+            got = look_up(lambda r: source[s, from_n, r : r + 1, :], row, column)
+            rec_out[n, :, pl.ds(s * kx, kx)] = jnp.where(live, got, 0.0).reshape(1, kx)
         box_out[:, pl.ds(s * kx, kx)] = land(slots, MOVES[s], 0).reshape(1, kx)
 
     pl.semaphore_wait(lower_in, len(beside))

time: 11.6 us -> 11.6 us (level)
  no operation moved by 1% of the time
where the time goes in v7:
time: 11.6 us; the launch traced here: 11.5 us
  Pallas kernels  10.8 us (93%)
  between operations  0.64 us (6%)
    pallas_call x1, Pallas kernels, per_device(): pl.pallas_call(functools.partial(body, (levels, cx, cy, sd, kx, ky, kc, n...  10.1 us
    pallas_call x1, Pallas kernels, per_device(): pl.pallas_call(publish, out_shape=tuple((jax.ShapeDtypeStruct(*s) for s i...  0.68 us

profile of v7, /device:TPU:0, one launch (start us, length us, event | category | flops | bytes accessed | tf_op | source)
XLA Modules:
  0.0 11.5 jit_solution(1524783285221626533)
XLA Ops:
  0.6 10.1 %shard_map.154 = (f32[2,8,128]{2,1,0:T(8,128)S(1)}, f32[2,8,128]{2,1,0:T(8,128)S(1)}, f32[128,128]{1,0:T(8,128)S(1)}, f32[128,128]{1,0:T(8,128)S(1)}, f32[5,1,2176]{2,1,0:T(1,128)S(1)}, /*index=5*/s32[1,2176]{1,0:T(1,128)S(1)}) custom-call(f32[2,8,128]{2,1,0:T(8,128)} %moist_in.1, f32[2,8,128]{2,1,0:T(8,128)} %warm_in.1, f32[128,128]{1,0:T(8,128)} %bitcast.8, ...), custom_call_target="tpu_custom_call" | custom-call | tf_op jit(solution)/shard_map/pallas_call | solution.py:736
  10.8 0.7 %shard_map.155 = (f32[2,8,128]{2,1,0:T(8,128)}, f32[2,8,128]{2,1,0:T(8,128)}, f32[128,128]{1,0:T(8,128)}, f32[128,128]{1,0:T(8,128)}, f32[5,1,2176]{2,1,0:T(1,128)}, /*index=5*/s32[1,2176]{1,0:T(1,128)}) custom-call(f32[2,8,128]{2,1,0:T(8,128)S(1)} %get-tuple-element.18.refs_0_, f32[2,8,128]{2,1,0:T(8,128)S(1)} %get-tuple-element.19.refs_1_, ...), custom_call_target="tpu_custom_call" | custom-call | tf_op jit(solution)/shard_map/pallas_call | solution.py:775

commit v8 on v7

--- a/solution.py
+++ b/solution.py
@@ -176,12 +176,8 @@
 
     def bring_rows(s, chosen, group):
         for n in chosen:
-            for l in range(levels):
-                stretch = pl.ds(l * sd, sd)
-                if n < 5:
-                    bring(cells[n].at[:, l, edges[s], :], row_pack.at[s, n, stretch, :], group)
-                else:
-                    bring(perm_cells.at[:, l, edges[s], :], turn_pack.at[s, stretch, :], group)
+            source = cells[n] if n < 5 else perm_cells
+            bring(source.at[:, :, edges[s], :], row_pack.at[s, n] if n < 5 else turn_pack.at[s], group)
 
     bring_rows(0, (5, 0, 1), 1)
     bring_rows(0, (2, 3, 4), 2)
@@ -247,9 +243,9 @@
     def sort_rows(s, chosen):
         for l in range(levels):
             stretch = pl.ds(l * sd, sd)
-            turns = turn_pack[s, stretch, :]
+            turns = turn_pack[s, :, l, :]
             for n in chosen:
-                row_sort[s, n, stretch, :] = take(row_pack[s, n, stretch, :], turns, 0)
+                row_sort[s, n, stretch, :] = take(row_pack[s, n, :, l, :], turns, 0)
 
     def send_first(s):
         sort_rows(s, (0, 1))
@@ -258,11 +254,13 @@
     def send_rows(s):
         sort_rows(s, (2, 3, 4))
         send(row_sort.at[s, 2:4], row_x.at[s, 2:4], (4, 3)[s], (MOVES[s], 0))
+
+    def send_rest(s):
         send(row_sort.at[s, 4], row_x.at[s, 4], (5, 3)[s], (MOVES[s], 0))
         for l in range(levels):
             rank = jnp.zeros((sd, cy), jnp.int32)
             for p in range(1, sd):
-                here = jnp.broadcast_to(turn_pack[s, l * sd + p : l * sd + p + 1, :], (sd, cy)) == seat
+                here = jnp.broadcast_to(turn_pack[s, p : p + 1, l, :], (sd, cy)) == seat
                 rank = jnp.where(here, p, rank)
             rank_of[s, pl.ds(l * sd, sd), :] = rank
         slots = list_pack[s].reshape(deep, cy)
@@ -277,8 +275,7 @@
         tile = None
         for n in range(6):
             for l in range(levels):
-                stretch = pl.ds(l * sd, sd)
-                value = row_pack[s, n, stretch, :] if n < 5 else turn_pack[s, stretch, :].astype(jnp.float32)
+                value = row_pack[s, n, :, l, :] if n < 5 else turn_pack[s, :, l, :].astype(jnp.float32)
                 spot = 8 * n + 4 * s + 2 * l
                 moved = turn(value, spot + 1, 1)
                 tile = moved if tile is None else jnp.where(lane >= spot, moved, tile)
@@ -302,9 +299,24 @@
     send_first(0)
     wait_rows(brought[2], in_sem.at[2])
     send_rows(0)
-    for copy in lists:
-        copy.wait()
-    send_corner(0)
+    before = sent[0], list(due)
+
+    @pl.when(me_y == 0)
+    def _():
+        send_rest(0)
+        for copy in lists:
+            copy.wait()
+        send_corner(0)
+
+    sent[0], due[:] = before
+
+    @pl.when(me_y != 0)
+    def _():
+        for copy in lists:
+            copy.wait()
+        send_corner(0)
+        send_rest(0)
+
     wait_rows(brought[0], in_sem.at[0])
     for t, dy in enumerate(ys):
         send(state, state_y.at[t], 0, (0, dy))
@@ -516,6 +528,7 @@
     send_fields(1)
     send_first(1)
     send_rows(1)
+    send_rest(1)
     send_corner(1)
 
     wait_rows(due[0], recv_sem.at[0])
@@ -750,10 +763,10 @@
             pltpu.VMEM((2, 1, kx), i32),
             pltpu.VMEM((2, 1, kx), i32),
             pltpu.VMEM((2, 1, kx), i32),
+            pltpu.VMEM((2, 5, sd, levels, cy), f32),
             pltpu.VMEM((2, 5, sd * levels, cy), f32),
             pltpu.VMEM((2, 5, sd * levels, cy), f32),
-            pltpu.VMEM((2, 5, sd * levels, cy), f32),
-            pltpu.VMEM((2, sd * levels, cy), i32),
+            pltpu.VMEM((2, sd, levels, cy), i32),
             pltpu.VMEM((2, sd * levels, cy), i32),
             pltpu.VMEM((2, sd, cy), f32),
             pltpu.VMEM((2, n_y, sd, cy), f32),

time: 11.6 us -> 11.7 us (level)
  no operation moved by 1% of the time
where the time goes in v8:
time: 11.7 us; the launch traced here: 11.5 us
  Pallas kernels  10.9 us (93%)
  between operations  0.64 us (5%)
    pallas_call x1, Pallas kernels, per_device(): pl.pallas_call(functools.partial(body, (levels, cx, cy, sd, kx, ky, kc, n...  10.2 us
    pallas_call x1, Pallas kernels, per_device(): pl.pallas_call(publish, out_shape=tuple((jax.ShapeDtypeStruct(*s) for s i...  0.68 us

profile of v8, /device:TPU:0, one launch (start us, length us, event | category | flops | bytes accessed | tf_op | source)
XLA Modules:
  0.0 11.5 jit_solution(5162757362229929249)
XLA Ops:
  0.6 10.2 %shard_map.154 = (f32[2,8,128]{2,1,0:T(8,128)S(1)}, f32[2,8,128]{2,1,0:T(8,128)S(1)}, f32[128,128]{1,0:T(8,128)S(1)}, f32[128,128]{1,0:T(8,128)S(1)}, f32[5,1,2176]{2,1,0:T(1,128)S(1)}, /*index=5*/s32[1,2176]{1,0:T(1,128)S(1)}) custom-call(f32[2,8,128]{2,1,0:T(8,128)} %moist_in.1, f32[2,8,128]{2,1,0:T(8,128)} %warm_in.1, f32[128,128]{1,0:T(8,128)} %bitcast.8, ...), custom_call_target="tpu_custom_call" | custom-call | tf_op jit(solution)/shard_map/pallas_call | solution.py:749
  10.8 0.7 %shard_map.155 = (f32[2,8,128]{2,1,0:T(8,128)}, f32[2,8,128]{2,1,0:T(8,128)}, f32[128,128]{1,0:T(8,128)}, f32[128,128]{1,0:T(8,128)}, f32[5,1,2176]{2,1,0:T(1,128)}, /*index=5*/s32[1,2176]{1,0:T(1,128)}) custom-call(f32[2,8,128]{2,1,0:T(8,128)S(1)} %get-tuple-element.18.refs_0_, f32[2,8,128]{2,1,0:T(8,128)S(1)} %get-tuple-element.19.refs_1_, ...), custom_call_target="tpu_custom_call" | custom-call | tf_op jit(solution)/shard_map/pallas_call | solution.py:788

commit v9 on v7

--- a/solution.py
+++ b/solution.py
@@ -196,12 +196,10 @@
 
     bring_rows(1, range(6), 0)
     bring(lx_in.at[0, pl.ds(1, 1), :], list_pack.at[1], 0)
-    lists = [
-        pltpu.make_async_copy(source.at[0], target, in_sem.at[3 + n])
-        for n, (source, target) in enumerate(((ly_in, ly), (lc_in, lc)))
-    ]
-    for copy in lists:
-        copy.start()
+    corner_list = pltpu.make_async_copy(lc_in.at[0], lc, in_sem.at[3])
+    corner_list.start()
+    face_list = pltpu.make_async_copy(ly_in.at[0], ly, in_sem.at[1])
+
     for n, source in enumerate((size_in, mult_in, dry_in, east_in, north_in)):
         bring(source, drops.at[n], 0)
     bring(perm_in, perm, 0)
@@ -300,10 +298,10 @@
         pl.semaphore_signal(lower_in, inc=1, device_id=at((1, dy)), device_id_type=MESH)
     wait_rows(brought[1], in_sem.at[1])
     send_first(0)
+    face_list.start()
     wait_rows(brought[2], in_sem.at[2])
     send_rows(0)
-    for copy in lists:
-        copy.wait()
+    corner_list.wait()
     send_corner(0)
     wait_rows(brought[0], in_sem.at[0])
     for t, dy in enumerate(ys):
@@ -319,6 +317,7 @@
                 moved = turn(value, spot + 1, 1)
                 tile = moved if tile is None else jnp.where(lane >= spot, moved, tile)
         col_pack[n] = tile
+    face_list.wait()
     for d in range(2):
         col_pack[6, d : d + 1, d * ky : (d + 1) * ky] = ly[d : d + 1, :].astype(jnp.float32)
     for t, dy in enumerate(ys):
@@ -768,7 +767,7 @@
             pltpu.VMEM((2, 2, sd * levels, cy), f32),
             pltpu.VMEM((3, levels, cx, cy), f32),
             pltpu.VMEM((levels, cx, cy), f32),
-            dma((5,)), dma((1,)), dma((7,)), pltpu.SemaphoreType.REGULAR,
+            dma((4,)), dma((1,)), dma((7,)), pltpu.SemaphoreType.REGULAR,
         ],
         compiler_params=pltpu.CompilerParams(collective_id=0, has_side_effects=True),
     )(moist, warm, *flat, size, mult, dry, east, north, perm, lx, ly, lc)

time: 11.6 us -> 11.7 us (level)
  no operation moved by 1% of the time
where the time goes in v9:
time: 11.7 us; the launch traced here: 11.6 us
  Pallas kernels  10.9 us (93%)
  between operations  0.64 us (5%)
    pallas_call x1, Pallas kernels, per_device(): pl.pallas_call(functools.partial(body, (levels, cx, cy, sd, kx, ky, kc, n...  10.2 us
    pallas_call x1, Pallas kernels, per_device(): pl.pallas_call(publish, out_shape=tuple((jax.ShapeDtypeStruct(*s) for s i...  0.68 us

profile of v9, /device:TPU:0, one launch (start us, length us, event | category | flops | bytes accessed | tf_op | source)
XLA Modules:
  0.0 11.6 jit_solution(8562169892838879440)
XLA Ops:
  0.6 10.2 %shard_map.154 = (f32[2,8,128]{2,1,0:T(8,128)S(1)}, f32[2,8,128]{2,1,0:T(8,128)S(1)}, f32[128,128]{1,0:T(8,128)S(1)}, f32[128,128]{1,0:T(8,128)S(1)}, f32[5,1,2176]{2,1,0:T(1,128)S(1)}, /*index=5*/s32[1,2176]{1,0:T(1,128)S(1)}) custom-call(f32[2,8,128]{2,1,0:T(8,128)} %moist_in.1, f32[2,8,128]{2,1,0:T(8,128)} %warm_in.1, f32[128,128]{1,0:T(8,128)} %bitcast.8, ...), custom_call_target="tpu_custom_call" | custom-call | tf_op jit(solution)/shard_map/pallas_call | solution.py:735
  10.9 0.7 %shard_map.155 = (f32[2,8,128]{2,1,0:T(8,128)}, f32[2,8,128]{2,1,0:T(8,128)}, f32[128,128]{1,0:T(8,128)}, f32[128,128]{1,0:T(8,128)}, f32[5,1,2176]{2,1,0:T(1,128)}, /*index=5*/s32[1,2176]{1,0:T(1,128)}) custom-call(f32[2,8,128]{2,1,0:T(8,128)S(1)} %get-tuple-element.18.refs_0_, f32[2,8,128]{2,1,0:T(8,128)S(1)} %get-tuple-element.19.refs_1_, ...), custom_call_target="tpu_custom_call" | custom-call | tf_op jit(solution)/shard_map/pallas_call | solution.py:774
